TPU v7x, 512 devices: a whole 4x8x8 slice. The times are simulated.
512 devices in a mesh: batch: 8 (over y_lo, x), rows: 8 (over z), chan: 8 (over y_hi, core).
Axes of the slice: x: 4, y: 8 (y_hi: 4, y_lo: 2; y = y_hi * 2 + y_lo), z: 8, core: 2. Of those that a mesh axis runs over, the one named last changes fastest.
Arguments:
- images: float32 [64, 24, 64, 32], P('batch', None, ('rows', 'chan')), may hold values from -6 to 6
- shift_mid: float32 [3, 24], replicated, may hold values from -1.75 to 1.75
- gain_mid: float32 [3, 24], replicated, may hold values from -0.3 to 0.3
- lower_mid: float32 [3, 24, 24], replicated, may hold values from -1.25 to 1.25
- upper_mid: float32 [3, 24, 24], replicated, may hold values from -1.25 to 1.25
- diag_mid: float32 [3, 24], replicated, may hold values from -0.3 to 0.3
- first_mid: bfloat16 [3, 9, 12, 512], replicated, may hold values from -0.625 to 0.625
- first_bias_mid: bfloat16 [3, 512], replicated, may hold values from -3 to 3
- second_mid: bfloat16 [3, 512, 512], replicated, may hold values from -0.25 to 0.25
- second_bias_mid: float32 [3, 512], replicated, may hold values from -3 to 3
- third_mid: bfloat16 [3, 9, 512, 24], replicated, may hold values from -0.09375 to 0.09375
- third_bias_mid: float32 [3, 24], replicated, may hold values from -3 to 3
- shift_top: float32 [2, 48], replicated, may hold values from -1.75 to 1.75
- gain_top: float32 [2, 48], replicated, may hold values from -0.3 to 0.3
- lower_top: float32 [2, 48, 48], replicated, may hold values from -0.875 to 0.875
- upper_top: float32 [2, 48, 48], replicated, may hold values from -0.875 to 0.875
- diag_top: float32 [2, 48], replicated, may hold values from -0.3 to 0.3
- first_top: bfloat16 [2, 9, 24, 512], replicated, may hold values from -0.4375 to 0.4375
- first_bias_top: bfloat16 [2, 512], replicated, may hold values from -3 to 3
- second_top: bfloat16 [2, 512, 512], replicated, may hold values from -0.25 to 0.25
- second_bias_top: float32 [2, 512], replicated, may hold values from -3 to 3
- third_top: bfloat16 [2, 9, 512, 48], replicated, may hold values from -0.09375 to 0.09375
- third_bias_top: float32 [2, 48], replicated, may hold values from -3 to 3
Outputs:
- latent_mid: float32 [64, 12, 64, 32], P('batch', None, ('rows', 'chan'))
- latent_top: float32 [64, 48, 32, 16], P(('batch', 'chan'), None, 'rows')
- loglik: float32 [64], P(('batch', 'chan'))
All inputs are finite; a program needn't handle non-finite values.
Results may differ from a plain program's by a relative error of at most 0.008.
Values may be sent and summed in bfloat16 or wider, within the bound.
No kernel may reach another device: no remote copies, remote signals or barrier semaphores. Data moves between devices by JAX's collectives and lax.ppermute only.
A program may use at most 64 MiB of HBM per device.

v0:
```python
import math

import jax
import jax.numpy as jnp
from jax import lax
from jax.sharding import PartitionSpec as P

log_two_pi = math.log(2.0 * math.pi)


def padded_2(x, sides, width):
    edges = {}
    for axis, dim in sides:
        size, length = (lax.axis_size(axis), x.shape[dim])
        up = [(i, (i + 1) % size) for i in range(size - 1)]
        last = lax.slice_in_dim(x, length - width, length, axis=dim)
        first = lax.slice_in_dim(x, 0, width, axis=dim)
        edges[dim] = (
            lax.ppermute(last, axis, up),
            lax.ppermute(first, axis, [(b, a) for a, b in up]),
        )
    done = []
    for _, dim in sides:
        low, high = edges[dim]
        around = [(width, width) if d in done else (0, 0) for d in range(x.ndim)]
        x = jnp.concatenate([jnp.pad(low, around), x, jnp.pad(high, around)], axis=dim)
        done.append(dim)
    return x


def with_halo(block, sides, width):
    for axis, dim in sides:
        count = lax.axis_size(axis)
        forward = [(i, i + 1) for i in range(count - 1)]
        backward = [(target, source) for source, target in forward]
        low = lax.ppermute(
            lax.slice_in_dim(block, block.shape[dim] - width, None, axis=dim), axis, forward
        )
        high = lax.ppermute(lax.slice_in_dim(block, 0, width, axis=dim), axis, backward)
        block = jnp.concatenate([low, block, high], axis=dim)
    return block


def in_blocks(x, dim, length):
    lengths = x.shape
    pieces = x.reshape(*lengths[:dim], length, lengths[dim] // length, *lengths[dim + 1 :])
    return jnp.moveaxis(pieces, dim, 0)


def summed_on_arrival(x, axis, dim):
    length = lax.axis_size(axis)
    pieces = lax.all_to_all(in_blocks(x, dim, length), axis, 0, 0, tiled=True)
    return jnp.sum(pieces, axis=0)


def sent_to_all(x, axis):
    copies = jnp.broadcast_to(x, (lax.axis_size(axis), *x.shape))
    return lax.all_to_all(copies, axis, split_axis=0, concat_axis=0, tiled=True)


def over_copies(x, axis):
    everything = sent_to_all(x, axis)
    return jnp.sum(everything, axis=0)


def conv_in(rimmed, weights, rows_out):
    columns = rimmed.shape[3]
    padded = jnp.pad(rimmed, ((0, 0), (0, 0), (0, 0), (1, 1)))
    summed = None
    for tap_idx in range(9):
        row_off = tap_idx // 3
        col_off = tap_idx % 3
        window = padded[:, :, row_off : row_off + rows_out, col_off : col_off + columns]
        contrib = jnp.einsum(
            "bchw,co->bhwo", window, weights[tap_idx], preferred_element_type=jnp.float32
        )
        summed = contrib if summed is None else summed + contrib
    return summed


def conv_out(rimmed, weights):
    rows_out = rimmed.shape[1] - 2
    columns = rimmed.shape[2]
    padded = jnp.pad(rimmed, ((0, 0), (0, 0), (1, 1), (0, 0)))
    summed = None
    for tap_idx in range(9):
        row_off = tap_idx // 3
        col_off = tap_idx % 3
        window = padded[:, row_off : row_off + rows_out, col_off : col_off + columns, :]
        contrib = jnp.einsum(
            "bhwc,co->bohw", window, weights[tap_idx], preferred_element_type=jnp.float32
        )
        summed = contrib if summed is None else summed + contrib
    return summed


def hidden_layers(widened, first_w, first_b, second_w, second_b, rows_out):
    inner = conv_in(widened, first_w, rows_out) + first_b.astype(jnp.float32)[None, None, None, :]
    inner = jax.nn.relu(inner).astype(jnp.bfloat16)
    middle = jnp.einsum("bhwc,co->bhwo", inner, second_w, preferred_element_type=jnp.float32)
    return jax.nn.relu(middle + second_b[None, None, None, :])


def mid_hidden(coupled, first_w, first_b, second_w, second_b):
    rimmed = padded_2(coupled, ((("rows", "chan"), 2),), 1)
    middle = hidden_layers(rimmed, first_w, first_b, second_w, second_b, coupled.shape[2]).astype(
        jnp.bfloat16
    )
    return padded_2(middle, ((("rows", "chan"), 1),), 1)


def top_hidden(coupled, first_w, first_b, second_w, second_b):
    rimmed = with_halo(coupled, (("rows", 2),), 1)
    middle = hidden_layers(rimmed, first_w, first_b, second_w, second_b, coupled.shape[2]).astype(
        jnp.bfloat16
    )
    return with_halo(middle, (("rows", 1),), 1)


def flow_step(flow_state, params, hidden_fn):
    (
        shift_vec,
        gain_vec,
        lower_raw,
        upper_raw,
        diag_log,
        first_w,
        first_b,
        second_w,
        second_b,
        third_w,
        third_b,
    ) = params
    channels = flow_state.shape[1]
    half_chan = channels // 2
    cell_count = flow_state.shape[2] * flow_state.shape[3]
    mixed_state = (flow_state + shift_vec[None, :, None, None]) * jnp.exp(gain_vec)[
        None, :, None, None
    ]
    lower_mat = jnp.tril(lower_raw, -1) + jnp.eye(channels, dtype=jnp.float32)
    upper_mat = jnp.triu(upper_raw, 1) + jnp.diag(jnp.exp(diag_log))
    matrix = jnp.dot(lower_mat, upper_mat, precision=lax.Precision.HIGHEST)
    mixed_state = jnp.einsum("oc,bchw->bohw", matrix, mixed_state, precision=lax.Precision.HIGHEST)
    part_a = mixed_state[:, :half_chan]
    part_b = mixed_state[:, half_chan:]
    coupled = part_a.astype(jnp.bfloat16)
    rim_middle = hidden_fn(coupled, first_w, first_b, second_w, second_b)
    output = conv_out(rim_middle, third_w) + third_b[None, :, None, None]
    gate_pre = output[:, :half_chan] + 2.0
    updated = (part_b + output[:, half_chan:]) * jax.nn.sigmoid(gate_pre)
    step_term = cell_count * (jnp.sum(gain_vec) + jnp.sum(diag_log)) + jnp.sum(
        jax.nn.log_sigmoid(gate_pre), axis=(1, 2, 3)
    )
    return (jnp.concatenate([part_a, updated], axis=1), step_term)


def scale_pass(flow_state, params, hidden_fn):
    logdet = jnp.zeros((flow_state.shape[0],), jnp.float32)
    for step_num in range(params[0].shape[0]):
        flow_state, step_term = flow_step(
            flow_state, tuple((p[step_num] for p in params)), hidden_fn
        )
        logdet = logdet + step_term
    return (flow_state, logdet)


def gauss_terms(latent):
    return -0.5 * jnp.sum(latent * latent, axis=(1, 2, 3)) - 0.5 * log_two_pi * latent[0].size


def body(
    images,
    shift_mid,
    gain_mid,
    lower_mid,
    upper_mid,
    diag_mid,
    first_mid,
    first_bias_mid,
    second_mid,
    second_bias_mid,
    third_mid,
    third_bias_mid,
    shift_top,
    gain_top,
    lower_top,
    upper_top,
    diag_top,
    first_top,
    first_bias_top,
    second_top,
    second_bias_top,
    third_top,
    third_bias_top,
):
    params_mid = (
        shift_mid,
        gain_mid,
        lower_mid,
        upper_mid,
        diag_mid,
        first_mid,
        first_bias_mid,
        second_mid,
        second_bias_mid,
        third_mid,
        third_bias_mid,
    )
    params_top = (
        shift_top,
        gain_top,
        lower_top,
        upper_top,
        diag_top,
        first_top,
        first_bias_top,
        second_top,
        second_bias_top,
        third_top,
        third_bias_top,
    )
    images_dev, channels, height, columns = images.shape
    flow_state, logdet_mid = scale_pass(images, params_mid, mid_hidden)
    half_chan = channels // 2
    latent_mid = flow_state[:, :half_chan]
    kept_chan = flow_state[:, half_chan:]
    mid_part = gauss_terms(latent_mid) + logdet_mid
    grouped = lax.all_to_all(kept_chan, "chan", split_axis=0, concat_axis=2, tiled=True)
    group_imgs, group_chan, group_rows, group_cols = grouped.shape
    squeezed = grouped.reshape(
        group_imgs, group_chan, group_rows // 2, 2, group_cols // 2, 2
    ).transpose(0, 1, 3, 5, 2, 4)
    squeezed = squeezed.reshape(group_imgs, group_chan * 4, group_rows // 2, group_cols // 2)
    latent_top, logdet_top = scale_pass(squeezed, params_top, top_hidden)
    top_part = gauss_terms(latent_top) + logdet_top
    mid_own = summed_on_arrival(mid_part, "chan", 0)
    summed = over_copies(mid_own + top_part, "rows")
    total_dims = channels * height * lax.axis_size("rows") * lax.axis_size("chan") * columns
    return (latent_mid, latent_top, summed / total_dims)


def solution(mesh):
    placed = (
        P("batch", None, ("rows", "chan"), None),
        P(),
        P(),
        P(),
        P(),
        P(),
        P(),
        P(),
        P(),
        P(),
        P(),
        P(),
        P(),
        P(),
        P(),
        P(),
        P(),
        P(),
        P(),
        P(),
        P(),
        P(),
        P(),
    )
    return jax.shard_map(
        body,
        mesh=mesh,
        in_specs=placed,
        out_specs=(
            P("batch", None, ("rows", "chan"), None),
            P(("batch", "chan"), None, "rows", None),
            P(("batch", "chan")),
        ),
        check_vma=False,
    )
```

profile of v0, /device:TPU:1, one launch (start us, length us, event | category | flops | bytes accessed | tf_op | source)
XLA Modules:
  0.0 222.2 jit_solution(14348905123432826290)
XLA Ops:
  5.2 5.6 %collective-permute-start = (bf16[8,12,1,32]{3,1,0,2:T(8,128)(2,1)S(1)}, bf16[8,12,1,32]{3,1,0,2:T(8,128)(2,1)S(1)}, u32[]{:S(2)}, u32[]{:S(2)}) collective-permute-start(bf16[8,12,1,32]{3,1,0,2:T(8,128)(2,1)S(1)} %slice.1913), channel_id=1, source_target_pairs={{0,1},{1,2},{2,3},{3,4},{4,5},{5,6},{6,7},{7,8},{8,9},{9,10},{10,1... | collective-permute-start | bytes 18440 | tf_op jit(solution)/shard_map/ppermute | solution.py:19
  10.8 4.4 %collective-permute-start.1 = (bf16[8,12,1,32]{3,1,0,2:T(8,128)(2,1)S(1)}, bf16[8,12,1,32]{3,1,0,2:T(8,128)(2,1)S(1)}, u32[]{:S(2)}, u32[]{:S(2)}) collective-permute-start(bf16[8,12,1,32]{3,1,0,2:T(8,128)(2,1)S(1)} %slice.1913), channel_id=1, source_target_pairs={{1,0},{2,1},{3,2},{4,3},{5,4},{6,5},{7,6},{8,7},{9,8},{10,9},{11,1... | collective-permute-start | bytes 18440 | tf_op jit(solution)/shard_map/ppermute | solution.py:20
  21.8 2.3 %collective-permute-start.2 = (bf16[8,1,32,512]{3,2,0,1:T(8,128)(2,1)S(1)}, bf16[8,1,32,512]{3,2,0,1:T(8,128)(2,1)S(1)}, u32[]{:S(2)}, u32[]{:S(2)}) collective-permute-start(bf16[8,1,32,512]{3,2,0,1:T(8,128)(2,1)S(1)} %bitcast.923), channel_id=1, source_target_pairs={{0,1},{1,2},{2,3},{3,4},{4,5},{5,6},{6,7},{7,8},{8,9},{9,10},{10,1... | collective-permute-start | bytes 786440 | tf_op jit(solution)/shard_map/ppermute | solution.py:19
  24.1 2.0 collective-permute-start.3
  27.4 10.4 %collective-permute-done.3 = bf16[8,1,32,512]{3,2,0,1:T(8,128)(2,1)S(1)} collective-permute-done((bf16[8,1,32,512]{3,2,0,1:T(8,128)(2,1)S(1)}, bf16[8,1,32,512]{3,2,0,1:T(8,128)(2,1)S(1)}, u32[]{:S(2)}, u32[]{:S(2)}) %collective-permute-start.3) | collective-permute-done | bytes 262176 | tf_op jit(solution)/shard_map/ppermute | solution.py:20
  50.0 2.4 %collective-permute-start.5 = (bf16[8,12,1,32]{3,1,0,2:T(8,128)(2,1)S(1)}, bf16[8,12,1,32]{3,1,0,2:T(8,128)(2,1)S(1)}, u32[]{:S(2)}, u32[]{:S(2)}) collective-permute-start(bf16[8,12,1,32]{3,1,0,2:T(8,128)(2,1)S(1)} %slice.1912), channel_id=1, source_target_pairs={{1,0},{2,1},{3,2},{4,3},{5,4},{6,5},{7,6},{8,7},{9,8},{10,9},{11,1... | collective-permute-start | bytes 18440 | tf_op jit(solution)/shard_map/ppermute | solution.py:20
  52.4 4.9 %collective-permute-done.5 = bf16[8,12,1,32]{3,1,0,2:T(8,128)(2,1)S(1)} collective-permute-done((bf16[8,12,1,32]{3,1,0,2:T(8,128)(2,1)S(1)}, bf16[8,12,1,32]{3,1,0,2:T(8,128)(2,1)S(1)}, u32[]{:S(2)}, u32[]{:S(2)}) %collective-permute-start.5) | collective-permute-done | bytes 6176 | tf_op jit(solution)/shard_map/ppermute | solution.py:20
  62.2 2.4 %collective-permute-start.7 = (bf16[8,1,32,512]{3,2,0,1:T(8,128)(2,1)S(1)}, bf16[8,1,32,512]{3,2,0,1:T(8,128)(2,1)S(1)}, u32[]{:S(2)}, u32[]{:S(2)}) collective-permute-start(bf16[8,1,32,512]{3,2,0,1:T(8,128)(2,1)S(1)} %bitcast.927), channel_id=1, source_target_pairs={{1,0},{2,1},{3,2},{4,3},{5,4},{6,5},{7,6},{8,7},{9,8},{10,9},{11,1... | collective-permute-start | bytes 786440 | tf_op jit(solution)/shard_map/ppermute | solution.py:20
  65.6 6.5 %collective-permute-done.7 = bf16[8,1,32,512]{3,2,0,1:T(8,128)(2,1)S(1)} collective-permute-done((bf16[8,1,32,512]{3,2,0,1:T(8,128)(2,1)S(1)}, bf16[8,1,32,512]{3,2,0,1:T(8,128)(2,1)S(1)}, u32[]{:S(2)}, u32[]{:S(2)}) %collective-permute-start.7) | collective-permute-done | bytes 262176 | tf_op jit(solution)/shard_map/ppermute | solution.py:20
  84.2 2.4 %collective-permute-start.9 = (bf16[8,12,1,32]{3,1,0,2:T(8,128)(2,1)S(1)}, bf16[8,12,1,32]{3,1,0,2:T(8,128)(2,1)S(1)}, u32[]{:S(2)}, u32[]{:S(2)}) collective-permute-start(bf16[8,12,1,32]{3,1,0,2:T(8,128)(2,1)S(1)} %slice.1916), channel_id=1, source_target_pairs={{1,0},{2,1},{3,2},{4,3},{5,4},{6,5},{7,6},{8,7},{9,8},{10,9},{11,1... | collective-permute-start | bytes 18440 | tf_op jit(solution)/shard_map/ppermute | solution.py:20
  87.4 4.5 %collective-permute-done.9 = bf16[8,12,1,32]{3,1,0,2:T(8,128)(2,1)S(1)} collective-permute-done((bf16[8,12,1,32]{3,1,0,2:T(8,128)(2,1)S(1)}, bf16[8,12,1,32]{3,1,0,2:T(8,128)(2,1)S(1)}, u32[]{:S(2)}, u32[]{:S(2)}) %collective-permute-start.9) | collective-permute-done | bytes 6176 | tf_op jit(solution)/shard_map/ppermute | solution.py:20
  96.7 2.4 %collective-permute-start.11 = (bf16[8,1,32,512]{3,2,0,1:T(8,128)(2,1)S(1)}, bf16[8,1,32,512]{3,2,0,1:T(8,128)(2,1)S(1)}, u32[]{:S(2)}, u32[]{:S(2)}) collective-permute-start(bf16[8,1,32,512]{3,2,0,1:T(8,128)(2,1)S(1)} %bitcast.930), channel_id=1, source_target_pairs={{1,0},{2,1},{3,2},{4,3},{5,4},{6,5},{7,6},{8,7},{9,8},{10,9},{11,1... | collective-permute-start | bytes 786440 | tf_op jit(solution)/shard_map/ppermute | solution.py:20
  100.1 8.0 %collective-permute-done.11 = bf16[8,1,32,512]{3,2,0,1:T(8,128)(2,1)S(1)} collective-permute-done((bf16[8,1,32,512]{3,2,0,1:T(8,128)(2,1)S(1)}, bf16[8,1,32,512]{3,2,0,1:T(8,128)(2,1)S(1)}, u32[]{:S(2)}, u32[]{:S(2)}) %collective-permute-start.11) | collective-permute-done | bytes 262176 | tf_op jit(solution)/shard_map/ppermute | solution.py:20
  119.9 7.8 %all-to-all-start = ((f32[8,1,384]{2,1,0:T(1,128)}), f32[8,1,384]{2,1,0:T(1,128)S(1)}, u32[]{:S(2)}, u32[]{:S(2)}) async-start(f32[8,1,384]{2,1,0:T(1,128)} %reshape.1494), calls=%async_computation | async-start | bytes 24576 | tf_op jit(solution)/shard_map/all_to_all | solution.py:228
  128.0 6.8 %all-to-all-done = f32[8,1,384]{2,1,0:T(1,128)S(1)} async-done(((f32[8,1,384]{2,1,0:T(1,128)}), f32[8,1,384]{2,1,0:T(1,128)S(1)}, u32[]{:S(2)}, u32[]{:S(2)}) %all-to-all-start) | async-done | bytes 12320 | tf_op jit(solution)/shard_map/all_to_all | solution.py:228
  136.3 4.0 %collective-permute-start.12 = (bf16[1,24,1,16]{1,3,2,0:T(8,128)(2,1)S(1)}, bf16[1,24,1,16]{1,3,2,0:T(8,128)(2,1)S(1)}, u32[]{:S(2)}, u32[]{:S(2)}) collective-permute-start(bf16[1,24,1,16]{1,3,2,0:T(8,128)(2,1)S(1)} %get-tuple-element.52), channel_id=1, source_target_pairs={{0,8},{8,16},{16,24},{24,32},{32,40},{40,48},{48,56},{1,9},{9,17},... | collective-permute-start | bytes 2312 | tf_op jit(solution)/shard_map/ppermute | solution.py:36
  141.6 3.7 %collective-permute-done.13 = bf16[1,24,1,16]{1,3,2,0:T(8,128)(2,1)S(1)} collective-permute-done((bf16[1,24,1,16]{1,3,2,0:T(8,128)(2,1)S(1)}, bf16[1,24,1,16]{1,3,2,0:T(8,128)(2,1)S(1)}, u32[]{:S(2)}, u32[]{:S(2)}) %collective-permute-start.13) | collective-permute-done | bytes 800 | tf_op jit(solution)/shard_map/ppermute | solution.py:39
  146.9 13.7 %collective-permute-start.14 = (bf16[1,1,16,512]{3,2,1,0:T(8,128)(2,1)S(1)}, bf16[1,1,16,512]{3,2,1,0:T(8,128)(2,1)S(1)}, u32[]{:S(2)}, u32[]{:S(2)}) collective-permute-start(bf16[1,1,16,512]{3,2,1,0:T(8,128)(2,1)S(1)} %get-tuple-element.42), channel_id=1, source_target_pairs={{0,8},{8,16},{16,24},{24,32},{32,40},{40,48},{48,56},{1,9},{9,17},... | collective-permute-start | bytes 49160 | tf_op jit(solution)/shard_map/ppermute | solution.py:36
  167.4 3.4 %collective-permute-start.16 = (bf16[1,24,1,16]{1,3,2,0:T(8,128)(2,1)S(1)}, bf16[1,24,1,16]{1,3,2,0:T(8,128)(2,1)S(1)}, u32[]{:S(2)}, u32[]{:S(2)}) collective-permute-start(bf16[1,24,1,16]{1,3,2,0:T(8,128)(2,1)S(1)} %get-tuple-element.50), channel_id=1, source_target_pairs={{0,8},{8,16},{16,24},{24,32},{32,40},{40,48},{48,56},{1,9},{9,17},... | collective-permute-start | bytes 2312 | tf_op jit(solution)/shard_map/ppermute | solution.py:36
  178.6 4.0 %collective-permute-start.18 = (bf16[1,1,16,512]{3,2,1,0:T(8,128)(2,1)S(1)}, bf16[1,1,16,512]{3,2,1,0:T(8,128)(2,1)S(1)}, u32[]{:S(2)}, u32[]{:S(2)}) collective-permute-start(bf16[1,1,16,512]{3,2,1,0:T(8,128)(2,1)S(1)} %get-tuple-element.40), channel_id=1, source_target_pairs={{0,8},{8,16},{16,24},{24,32},{32,40},{40,48},{48,56},{1,9},{9,17},... | collective-permute-start | bytes 49160 | tf_op jit(solution)/shard_map/ppermute | solution.py:36
  184.6 7.6 %all-to-all-start.1 = ((f32[8,1,1]{2,1,0:T(1,128)}), f32[8,1,1]{2,1,0:T(1,128)S(1)}, u32[]{:S(2)}, u32[]{:S(2)}) async-start(f32[8,1,1]{2,1,0:T(1,128)} %copy.48), calls=%async_computation.1 | async-start | bytes 8192 | tf_op jit(solution)/shard_map/all_to_all | solution.py:52
  192.2 7.0 %all-to-all-done.1 = f32[8,1,1]{2,1,0:T(1,128)S(1)} async-done(((f32[8,1,1]{2,1,0:T(1,128)}), f32[8,1,1]{2,1,0:T(1,128)S(1)}, u32[]{:S(2)}, u32[]{:S(2)}) %all-to-all-start.1) | async-done | bytes 64 | tf_op jit(solution)/shard_map/all_to_all | solution.py:52
  206.4 6.8 %all-to-all-start.2 = ((f32[8,1,1]{2,1,0:T(1,128)}), f32[8,1,1]{2,1,0:T(1,128)S(1)}, u32[]{:S(2)}, u32[]{:S(2)}) async-start(f32[8,1,1]{2,1,0:T(1,128)} %broadcast_in_dim.91), calls=%async_computation.2 | async-start | bytes 8192 | tf_op jit(solution)/shard_map/all_to_all | solution.py:58
  213.9 5.9 %all-to-all-done.2 = f32[8,1,1]{2,1,0:T(1,128)S(1)} async-done(((f32[8,1,1]{2,1,0:T(1,128)}), f32[8,1,1]{2,1,0:T(1,128)S(1)}, u32[]{:S(2)}, u32[]{:S(2)}) %all-to-all-start.2) | async-done | bytes 64 | tf_op jit(solution)/shard_map/all_to_all | solution.py:58
  (203 shorter events, 80.7 us)
Async XLA Ops:
  5.2 11.7 %collective-permute-start = (bf16[8,12,1,32]{3,1,0,2:T(8,128)(2,1)S(1)}, bf16[8,12,1,32]{3,1,0,2:T(8,128)(2,1)S(1)}, u32[]{:S(2)}, u32[]{:S(2)}) collective-permute-start(bf16[8,12,1,32]{3,1,0,2:T(8,128)(2,1)S(1)} %slice.1913), channel_id=1, source_target_pairs={{0,1},{1,2},{2,3},{3,4},{4,5},{5,6},{6,7},{7,8},{8,9},{9,10},{10,1... | collective-permute-start | bytes 18440 | tf_op jit(solution)/shard_map/ppermute | solution.py:19
  10.8 6.1 %collective-permute-start.1 = (bf16[8,12,1,32]{3,1,0,2:T(8,128)(2,1)S(1)}, bf16[8,12,1,32]{3,1,0,2:T(8,128)(2,1)S(1)}, u32[]{:S(2)}, u32[]{:S(2)}) collective-permute-start(bf16[8,12,1,32]{3,1,0,2:T(8,128)(2,1)S(1)} %slice.1913), channel_id=1, source_target_pairs={{1,0},{2,1},{3,2},{4,3},{5,4},{6,5},{7,6},{8,7},{9,8},{10,9},{11,1... | collective-permute-start | bytes 18440 | tf_op jit(solution)/shard_map/ppermute | solution.py:20
  21.8 5.6 %collective-permute-start.2 = (bf16[8,1,32,512]{3,2,0,1:T(8,128)(2,1)S(1)}, bf16[8,1,32,512]{3,2,0,1:T(8,128)(2,1)S(1)}, u32[]{:S(2)}, u32[]{:S(2)}) collective-permute-start(bf16[8,1,32,512]{3,2,0,1:T(8,128)(2,1)S(1)} %bitcast.923), channel_id=1, source_target_pairs={{0,1},{1,2},{2,3},{3,4},{4,5},{5,6},{6,7},{7,8},{8,9},{9,10},{10,1... | collective-permute-start | bytes 786440 | tf_op jit(solution)/shard_map/ppermute | solution.py:19
  24.1 13.7 %collective-permute-start.3 = (bf16[8,1,32,512]{3,2,0,1:T(8,128)(2,1)S(1)}, bf16[8,1,32,512]{3,2,0,1:T(8,128)(2,1)S(1)}, u32[]{:S(2)}, u32[]{:S(2)}) collective-permute-start(bf16[8,1,32,512]{3,2,0,1:T(8,128)(2,1)S(1)} %bitcast.924), channel_id=1, source_target_pairs={{1,0},{2,1},{3,2},{4,3},{5,4},{6,5},{7,6},{8,7},{9,8},{10,9},{11,1... | collective-permute-start | bytes 786440 | tf_op jit(solution)/shard_map/ppermute | solution.py:20
  48.1 4.4 %collective-permute-start.4 = (bf16[8,12,1,32]{3,1,0,2:T(8,128)(2,1)S(1)}, bf16[8,12,1,32]{3,1,0,2:T(8,128)(2,1)S(1)}, u32[]{:S(2)}, u32[]{:S(2)}) collective-permute-start(bf16[8,12,1,32]{3,1,0,2:T(8,128)(2,1)S(1)} %slice.1912), channel_id=1, source_target_pairs={{0,1},{1,2},{2,3},{3,4},{4,5},{5,6},{6,7},{7,8},{8,9},{9,10},{10,1... | collective-permute-start | bytes 18440 | tf_op jit(solution)/shard_map/ppermute | solution.py:19
  50.0 7.3 %collective-permute-start.5 = (bf16[8,12,1,32]{3,1,0,2:T(8,128)(2,1)S(1)}, bf16[8,12,1,32]{3,1,0,2:T(8,128)(2,1)S(1)}, u32[]{:S(2)}, u32[]{:S(2)}) collective-permute-start(bf16[8,12,1,32]{3,1,0,2:T(8,128)(2,1)S(1)} %slice.1912), channel_id=1, source_target_pairs={{1,0},{2,1},{3,2},{4,3},{5,4},{6,5},{7,6},{8,7},{9,8},{10,9},{11,1... | collective-permute-start | bytes 18440 | tf_op jit(solution)/shard_map/ppermute | solution.py:20
  60.2 5.3 %collective-permute-start.6 = (bf16[8,1,32,512]{3,2,0,1:T(8,128)(2,1)S(1)}, bf16[8,1,32,512]{3,2,0,1:T(8,128)(2,1)S(1)}, u32[]{:S(2)}, u32[]{:S(2)}) collective-permute-start(bf16[8,1,32,512]{3,2,0,1:T(8,128)(2,1)S(1)} %bitcast.926), channel_id=1, source_target_pairs={{0,1},{1,2},{2,3},{3,4},{4,5},{5,6},{6,7},{7,8},{8,9},{9,10},{10,1... | collective-permute-start | bytes 786440 | tf_op jit(solution)/shard_map/ppermute | solution.py:19
  62.2 9.9 %collective-permute-start.7 = (bf16[8,1,32,512]{3,2,0,1:T(8,128)(2,1)S(1)}, bf16[8,1,32,512]{3,2,0,1:T(8,128)(2,1)S(1)}, u32[]{:S(2)}, u32[]{:S(2)}) collective-permute-start(bf16[8,1,32,512]{3,2,0,1:T(8,128)(2,1)S(1)} %bitcast.927), channel_id=1, source_target_pairs={{1,0},{2,1},{3,2},{4,3},{5,4},{6,5},{7,6},{8,7},{9,8},{10,9},{11,1... | collective-permute-start | bytes 786440 | tf_op jit(solution)/shard_map/ppermute | solution.py:20
  82.3 5.1 %collective-permute-start.8 = (bf16[8,12,1,32]{3,1,0,2:T(8,128)(2,1)S(1)}, bf16[8,12,1,32]{3,1,0,2:T(8,128)(2,1)S(1)}, u32[]{:S(2)}, u32[]{:S(2)}) collective-permute-start(bf16[8,12,1,32]{3,1,0,2:T(8,128)(2,1)S(1)} %slice.1916), channel_id=1, source_target_pairs={{0,1},{1,2},{2,3},{3,4},{4,5},{5,6},{6,7},{7,8},{8,9},{9,10},{10,1... | collective-permute-start | bytes 18440 | tf_op jit(solution)/shard_map/ppermute | solution.py:19
  84.2 7.7 %collective-permute-start.9 = (bf16[8,12,1,32]{3,1,0,2:T(8,128)(2,1)S(1)}, bf16[8,12,1,32]{3,1,0,2:T(8,128)(2,1)S(1)}, u32[]{:S(2)}, u32[]{:S(2)}) collective-permute-start(bf16[8,12,1,32]{3,1,0,2:T(8,128)(2,1)S(1)} %slice.1916), channel_id=1, source_target_pairs={{1,0},{2,1},{3,2},{4,3},{5,4},{6,5},{7,6},{8,7},{9,8},{10,9},{11,1... | collective-permute-start | bytes 18440 | tf_op jit(solution)/shard_map/ppermute | solution.py:20
  94.8 5.3 %collective-permute-start.10 = (bf16[8,1,32,512]{3,2,0,1:T(8,128)(2,1)S(1)}, bf16[8,1,32,512]{3,2,0,1:T(8,128)(2,1)S(1)}, u32[]{:S(2)}, u32[]{:S(2)}) collective-permute-start(bf16[8,1,32,512]{3,2,0,1:T(8,128)(2,1)S(1)} %bitcast.929), channel_id=1, source_target_pairs={{0,1},{1,2},{2,3},{3,4},{4,5},{5,6},{6,7},{7,8},{8,9},{9,10},{10,1... | collective-permute-start | bytes 786440 | tf_op jit(solution)/shard_map/ppermute | solution.py:19
  96.7 11.4 %collective-permute-start.11 = (bf16[8,1,32,512]{3,2,0,1:T(8,128)(2,1)S(1)}, bf16[8,1,32,512]{3,2,0,1:T(8,128)(2,1)S(1)}, u32[]{:S(2)}, u32[]{:S(2)}) collective-permute-start(bf16[8,1,32,512]{3,2,0,1:T(8,128)(2,1)S(1)} %bitcast.930), channel_id=1, source_target_pairs={{1,0},{2,1},{3,2},{4,3},{5,4},{6,5},{7,6},{8,7},{9,8},{10,9},{11,1... | collective-permute-start | bytes 786440 | tf_op jit(solution)/shard_map/ppermute | solution.py:20
  114.8 30.5 %copy-start.3 = (bf16[2,9,24,512]{3,2,1,0:T(8,128)(2,1)S(1)}, bf16[2,9,24,512]{3,2,1,0:T(8,128)(2,1)}, u32[]{:S(2)}) copy-start(bf16[2,9,24,512]{3,2,1,0:T(8,128)(2,1)} %param.40) | copy-start | bytes 1327108
  119.9 14.9 %all-to-all-start = ((f32[8,1,384]{2,1,0:T(1,128)}), f32[8,1,384]{2,1,0:T(1,128)S(1)}, u32[]{:S(2)}, u32[]{:S(2)}) async-start(f32[8,1,384]{2,1,0:T(1,128)} %reshape.1494), calls=%async_computation | async-start | bytes 24576 | tf_op jit(solution)/shard_map/all_to_all | solution.py:228
  136.3 5.3 %collective-permute-start.12 = (bf16[1,24,1,16]{1,3,2,0:T(8,128)(2,1)S(1)}, bf16[1,24,1,16]{1,3,2,0:T(8,128)(2,1)S(1)}, u32[]{:S(2)}, u32[]{:S(2)}) collective-permute-start(bf16[1,24,1,16]{1,3,2,0:T(8,128)(2,1)S(1)} %get-tuple-element.52), channel_id=1, source_target_pairs={{0,8},{8,16},{16,24},{24,32},{32,40},{40,48},{48,56},{1,9},{9,17},... | collective-permute-start | bytes 2312 | tf_op jit(solution)/shard_map/ppermute | solution.py:36
  140.3 5.0 %collective-permute-start.13 = (bf16[1,24,1,16]{1,3,2,0:T(8,128)(2,1)S(1)}, bf16[1,24,1,16]{1,3,2,0:T(8,128)(2,1)S(1)}, u32[]{:S(2)}, u32[]{:S(2)}) collective-permute-start(bf16[1,24,1,16]{1,3,2,0:T(8,128)(2,1)S(1)} %get-tuple-element.53), channel_id=1, source_target_pairs={{8,0},{16,8},{24,16},{32,24},{40,32},{48,40},{56,48},{9,1},{17,9},... | collective-permute-start | bytes 2312 | tf_op jit(solution)/shard_map/ppermute | solution.py:39
  146.9 16.5 %collective-permute-start.14 = (bf16[1,1,16,512]{3,2,1,0:T(8,128)(2,1)S(1)}, bf16[1,1,16,512]{3,2,1,0:T(8,128)(2,1)S(1)}, u32[]{:S(2)}, u32[]{:S(2)}) collective-permute-start(bf16[1,1,16,512]{3,2,1,0:T(8,128)(2,1)S(1)} %get-tuple-element.42), channel_id=1, source_target_pairs={{0,8},{8,16},{16,24},{24,32},{32,40},{40,48},{48,56},{1,9},{9,17},... | collective-permute-start | bytes 49160 | tf_op jit(solution)/shard_map/ppermute | solution.py:36
  160.6 4.5 %collective-permute-start.15 = (bf16[1,1,16,512]{3,2,1,0:T(8,128)(2,1)S(1)}, bf16[1,1,16,512]{3,2,1,0:T(8,128)(2,1)S(1)}, u32[]{:S(2)}, u32[]{:S(2)}) collective-permute-start(bf16[1,1,16,512]{3,2,1,0:T(8,128)(2,1)S(1)} %get-tuple-element.43), channel_id=1, source_target_pairs={{8,0},{16,8},{24,16},{32,24},{40,32},{48,40},{56,48},{9,1},{17,9},... | collective-permute-start | bytes 49160 | tf_op jit(solution)/shard_map/ppermute | solution.py:39
  167.4 9.7 %collective-permute-start.16 = (bf16[1,24,1,16]{1,3,2,0:T(8,128)(2,1)S(1)}, bf16[1,24,1,16]{1,3,2,0:T(8,128)(2,1)S(1)}, u32[]{:S(2)}, u32[]{:S(2)}) collective-permute-start(bf16[1,24,1,16]{1,3,2,0:T(8,128)(2,1)S(1)} %get-tuple-element.50), channel_id=1, source_target_pairs={{0,8},{8,16},{16,24},{24,32},{32,40},{40,48},{48,56},{1,9},{9,17},... | collective-permute-start | bytes 2312 | tf_op jit(solution)/shard_map/ppermute | solution.py:36
  170.8 6.3 %collective-permute-start.17 = (bf16[1,24,1,16]{1,3,2,0:T(8,128)(2,1)S(1)}, bf16[1,24,1,16]{1,3,2,0:T(8,128)(2,1)S(1)}, u32[]{:S(2)}, u32[]{:S(2)}) collective-permute-start(bf16[1,24,1,16]{1,3,2,0:T(8,128)(2,1)S(1)} %get-tuple-element.51), channel_id=1, source_target_pairs={{8,0},{16,8},{24,16},{32,24},{40,32},{48,40},{56,48},{9,1},{17,9},... | collective-permute-start | bytes 2312 | tf_op jit(solution)/shard_map/ppermute | solution.py:39
  178.6 21.8 %collective-permute-start.18 = (bf16[1,1,16,512]{3,2,1,0:T(8,128)(2,1)S(1)}, bf16[1,1,16,512]{3,2,1,0:T(8,128)(2,1)S(1)}, u32[]{:S(2)}, u32[]{:S(2)}) collective-permute-start(bf16[1,1,16,512]{3,2,1,0:T(8,128)(2,1)S(1)} %get-tuple-element.40), channel_id=1, source_target_pairs={{0,8},{8,16},{16,24},{24,32},{32,40},{40,48},{48,56},{1,9},{9,17},... | collective-permute-start | bytes 49160 | tf_op jit(solution)/shard_map/ppermute | solution.py:36
  182.6 17.8 %collective-permute-start.19 = (bf16[1,1,16,512]{3,2,1,0:T(8,128)(2,1)S(1)}, bf16[1,1,16,512]{3,2,1,0:T(8,128)(2,1)S(1)}, u32[]{:S(2)}, u32[]{:S(2)}) collective-permute-start(bf16[1,1,16,512]{3,2,1,0:T(8,128)(2,1)S(1)} %get-tuple-element.41), channel_id=1, source_target_pairs={{8,0},{16,8},{24,16},{32,24},{40,32},{48,40},{56,48},{9,1},{17,9},... | collective-permute-start | bytes 49160 | tf_op jit(solution)/shard_map/ppermute | solution.py:39
  184.6 14.6 %all-to-all-start.1 = ((f32[8,1,1]{2,1,0:T(1,128)}), f32[8,1,1]{2,1,0:T(1,128)S(1)}, u32[]{:S(2)}, u32[]{:S(2)}) async-start(f32[8,1,1]{2,1,0:T(1,128)} %copy.48), calls=%async_computation.1 | async-start | bytes 8192 | tf_op jit(solution)/shard_map/all_to_all | solution.py:52
  206.4 13.4 %all-to-all-start.2 = ((f32[8,1,1]{2,1,0:T(1,128)}), f32[8,1,1]{2,1,0:T(1,128)S(1)}, u32[]{:S(2)}, u32[]{:S(2)}) async-start(f32[8,1,1]{2,1,0:T(1,128)} %broadcast_in_dim.91), calls=%async_computation.2 | async-start | bytes 8192 | tf_op jit(solution)/shard_map/all_to_all | solution.py:58
  (14 other events, 173.2 us)
where the time goes:
time: 226 us; the launch traced here: 222 us
  starting transfers between devices  84.2 us (37%)
  waiting for transfers between devices  60.7 us (27%)
  matrix products  47.6 us (21%)
  between operations  12.4 us (5%)
  other arithmetic  11.4 us (5%)
  local copies, waits for them, and re-layouts  5.92 us (3%)
    ppermute x6, waiting for transfers between devices, padded_2(): lax.ppermute(first, axis, [(b, a) for a, b in up])  34.4 us
    dot_general x45, matrix products, conv_out(): jnp.einsum('bhwc,co->bohw', window, weights[tap_idx], preferred_element_t...  30.4 us
    ppermute x4, starting transfers between devices, with_halo(): lax.ppermute(lax.slice_in_dim(block, block.shape[dim] - width, None, axis...  25 us
    ppermute x6, starting transfers between devices, padded_2(): lax.ppermute(first, axis, [(b, a) for a, b in up])  16.1 us
    ppermute x6, starting transfers between devices, padded_2(): lax.ppermute(last, axis, up)  15.6 us
    dot_general x40, matrix products, conv_in(): jnp.einsum('bchw,co->bhwo', window, weights[tap_idx], preferred_element_t...  10.6 us
    all_to_all x1, starting transfers between devices, body(): lax.all_to_all(kept_chan, 'chan', split_axis=0, concat_axis=2, tiled=True)  7.84 us
    all_to_all x1, starting transfers between devices, summed_on_arrival(): pieces = lax.all_to_all(in_blocks(x, dim, length), axis, 0, 0, tiled=True)  7.61 us
  transfers between devices with their start and end apart: 23, of which 13 were waited for; matrix products, arithmetic and copies ran while one was open for 3% of the time, Pallas kernels for 0%

commit v1 on v0

v1 whole, which is shorter than its diff:
```python
import functools
import math

import jax
import jax.numpy as jnp
from jax import lax
from jax.experimental import pallas as pl
from jax.experimental.pallas import tpu as pltpu
from jax.sharding import PartitionSpec as P

BF = jnp.bfloat16
F32 = jnp.float32
log_two_pi = math.log(2.0 * math.pi)
VMEM = pl.BlockSpec(memory_space=pltpu.VMEM)
SMEM = pl.BlockSpec(memory_space=pltpu.SMEM)


def iota(shape, dim):
    return lax.broadcasted_iota(jnp.int32, shape, dim)


def eye(n, dtype):
    return (iota((n, n), 0) == iota((n, n), 1)).astype(dtype)


def dot_t(a, b):
    return lax.dot_general(a, b, (((1,), (1,)), ((), ())), preferred_element_type=F32)


def dot(a, b):
    return jnp.dot(a, b, preferred_element_type=F32)


def halves(x):
    high = x.astype(BF)
    return high, (x - high.astype(F32)).astype(BF)


def to_column(row):
    n = row.shape[1]
    same = iota((n, n), 0) == iota((n, n), 1)
    return jnp.sum(jnp.where(same, row, 0.0), axis=1, keepdims=True)


def three_term_left(matrix):
    high, low = halves(matrix)
    return jnp.concatenate([high, high, low], axis=1)


def select_rows(n_out, n_in, source_of):
    return (iota((n_out, n_in), 1) == source_of(iota((n_out, n_in), 0))).astype(F32)


def spread_mid(o):
    return jnp.where(o < 12, o, jnp.where(o >= 20, o - 8, -1))


def flow_matrix(gain, lower, upper, diag, shift, n):
    i, j = iota((n, n), 0), iota((n, n), 1)
    low = jnp.where(i > j, lower, 0.0) + jnp.where(i == j, 1.0, 0.0)
    up = jnp.where(i < j, upper, 0.0) + jnp.where(i == j, jnp.exp(diag), 0.0)
    matrix = jnp.dot(low, up, precision=lax.Precision.HIGHEST, preferred_element_type=F32)
    matrix = matrix * jnp.exp(gain)
    return matrix, jnp.sum(matrix * shift, axis=1, keepdims=True)


def exact_dot(a, b):
    return jnp.dot(a, b, precision=lax.Precision.HIGHEST, preferred_element_type=F32)


def prep_kernel(
    shift_mid, gain_mid, lower_mid, upper_mid, diag_mid, first_mid, first_bias_mid, second_mid,
    second_bias_mid, third_mid, third_bias_mid,
    shift_top, gain_top, lower_top, upper_top, diag_top, first_top, first_bias_top, second_top,
    second_bias_top, third_top, third_bias_top,
    a_mid, bu_mid, w1_mid, w2_mid, b2_mid, w3_mid, b3_mid,
    a_top0, a_top1, bu_top, w1_top, w2_top, b2_top, w3_top, b3_top, const,
):
    hid = second_mid.shape[1]
    ident = eye(hid, BF)
    total = jnp.zeros((1, 1), F32)
    for s in range(3):
        row = slice(s, s + 1)
        matrix, offset = flow_matrix(gain_mid[row], lower_mid[s], upper_mid[s], diag_mid[row], shift_mid[row], 24)
        total = total + 2048.0 * jnp.sum(gain_mid[row] + diag_mid[row], axis=1, keepdims=True)
        rows = select_rows(32, 24, spread_mid)
        matrix = exact_dot(rows, matrix)
        offset = jnp.sum(rows * jnp.sum(jnp.where(eye(24, F32) > 0, offset, 0.0), axis=0, keepdims=True), axis=1, keepdims=True)
        offset = offset + (iota((32, 1), 0) == 12).astype(F32)
        if s == 0:
            columns = (iota((24, 32), 0) == iota((24, 32), 1)).astype(F32)
        else:
            columns = (iota((24, 32), 0) == spread_mid(iota((24, 32), 1))).astype(F32)
        a_mid[s] = three_term_left(exact_dot(matrix, columns))
        bu_mid[s] = jnp.broadcast_to(offset, (32, 128))
        zeros = jnp.zeros((4, hid), F32)
        with_bias = jnp.concatenate([first_bias_mid[row].astype(F32), zeros[:3]], axis=0)
        blocks = []
        for tap in range(9):
            blocks += [first_mid[s, tap].astype(F32), with_bias if tap == 4 else zeros]
        w1_mid[s] = dot_t(ident, jnp.concatenate(blocks, axis=0).astype(BF)).astype(BF)
        w2_mid[s] = dot_t(ident, second_mid[s]).astype(BF)
        b2_mid[s] = jnp.broadcast_to(second_bias_mid[row], (128, hid)).T
        for tap in range(9):
            w3_mid[s, 24 * tap : 24 * tap + 24, :] = dot_t(eye(24, BF), third_mid[s, tap]).astype(BF)
        b3 = to_column(third_bias_mid[row]) + jnp.where(iota((24, 1), 0) < 12, 2.0, 0.0)
        b3_mid[s] = jnp.broadcast_to(b3, (24, 128))
    for s in range(2):
        row = slice(s, s + 1)
        matrix, offset = flow_matrix(gain_top[row], lower_top[s], upper_top[s], diag_top[row], shift_top[row], 48)
        total = total + 512.0 * jnp.sum(gain_top[row] + diag_top[row], axis=1, keepdims=True)
        if s == 0:
            k = iota((48, 64), 1)
            source = jnp.where(k % 16 >= 4, 4 * (k % 16 - 4) + k // 16, -1)
            a_top0[...] = three_term_left(exact_dot(matrix, (iota((48, 64), 0) == source).astype(F32)))
        else:
            a_top1[...] = three_term_left(matrix)
        bu_top[s] = jnp.broadcast_to(offset, (48, 128))
        blocks = [first_top[s, tap].astype(F32) for tap in range(9)]
        blocks += [first_bias_top[row].astype(F32), jnp.zeros((7, hid), F32)]
        w1_top[s] = dot_t(ident, jnp.concatenate(blocks, axis=0).astype(BF)).astype(BF)
        w2_top[s] = dot_t(ident, second_top[s]).astype(BF)
        b2_top[s] = jnp.broadcast_to(second_bias_top[row], (128, hid)).T
        for tap in range(9):
            w3_top[s, 48 * tap : 48 * tap + 48, :] = dot_t(eye(48, BF), third_top[s, tap]).astype(BF)
        b3 = to_column(third_bias_top[row]) + jnp.where(iota((48, 1), 0) < 24, 2.0, 0.0)
        b3_top[s] = jnp.broadcast_to(b3, (48, 128))
    const[...] = jnp.broadcast_to(total, (8, 128))


def tiled(column, lanes):
    return jnp.concatenate([column] * (lanes // 128), axis=1)


def moved(x, by):
    lanes = x.shape[1]
    return pltpu.roll(x, (-by) % lanes, 1)


def row_moved(x, dr, width):
    if dr == 0:
        return x
    lane = iota(x.shape, 1)
    inside = lane >= width if dr < 0 else lane < x.shape[1] - width
    return jnp.where(inside, moved(x, dr * width), 0.0)


def column_moved(x, dc, width):
    if dc == 0:
        return x
    column = iota(x.shape, 1) % width
    inside = column >= 1 if dc < 0 else column <= width - 2
    return jnp.where(inside, moved(x, dc), 0.0)


def conditioner(q, extra, w1, w2, b2, w3, b3, x_scr, p_scr, width, chunk):
    cells = q.shape[1]
    rows = q.shape[0]
    sides = [column_moved(q, dc, width) for dc in (-1, 0, 1)]
    blocks = [row_moved(side, dr, width) for dr in (-1, 0, 1) for side in sides]
    if extra is not None:
        blocks.append(extra)
    x_scr[...] = jnp.concatenate(blocks, axis=0).astype(BF)
    bias = tiled(b2, chunk)

    def one(i):
        at = pl.ds(i * chunk, chunk)
        inner = jnp.maximum(dot(w1, x_scr[:, at]), 0.0).astype(BF)
        middle = jnp.maximum(dot(w2, inner) + bias, 0.0).astype(BF)
        p_scr[:, at] = dot(w3, middle)

    for i in range(cells // chunk):
        one(i)
    n_out = p_scr.shape[0] // 9
    out = tiled(b3, cells)
    for dc in (-1, 0, 1):
        part = None
        for dr in (-1, 0, 1):
            tap = 3 * (dr + 1) + dc + 1
            term = row_moved(p_scr[n_out * tap : n_out * (tap + 1), :], dr, width)
            part = term if part is None else part + term
        out = out + column_moved(part, dc, width)
    return out


def gate_of(g):
    e = jnp.exp(-jnp.abs(g))
    scale = 1.0 / (1.0 + e)
    return jnp.where(g >= 0.0, scale, e * scale), jnp.minimum(g, 0.0) - jnp.log(1.0 + e)


def mix(a, parts, bias):
    return dot(a, jnp.concatenate(parts, axis=0)) + bias


def mid_update(u, s, refs, x_scr, p_scr):
    w1, w2, b2, w3, b3 = refs
    out = conditioner(u[:16], None, w1[s], w2[s], b2[s], w3[s], b3[s], x_scr, p_scr, 32, 512)
    scale, logs = gate_of(out[:16])
    logs = jnp.where(iota(logs.shape, 0) < 12, logs, 0.0)
    updated = (u[16:] + out[8:]) * pltpu.roll(scale, 4, 0)
    return updated, jnp.sum(logs, keepdims=True)


def mid_kernel(slots, where, a_mid, bu_mid, w1, w2, b2, w3, b3, u_out, sum_out, latent_out, x_scr, p_scr):
    refs = (w1, w2, b2, w3, b3)
    cells = 2048
    lane = iota((8, 128), 1) // 32
    groups = []
    for g in range(3):
        pieces = []
        for k in range(16):
            piece = None
            for j in range(4):
                source = slots[4 * k + j]
                turn = (32 * (j - g)) % 128
                source = pltpu.roll(source, turn, 1) if turn else source
                piece = source if piece is None else jnp.where(lane == j, source, piece)
            pieces.append(piece)
        groups.append(jnp.concatenate(pieces, axis=1))
    state = jnp.concatenate(groups + [jnp.zeros((8, cells), F32)], axis=0)
    total = jnp.zeros((1, 1), F32)
    for s in range(2):
        high, low = halves(state)
        u = mix(a_mid[s], [high, low, high], tiled(bu_mid[s], cells))
        updated, logs = mid_update(u, s, refs, x_scr, p_scr)
        total = total + logs
        state = jnp.concatenate([u[:16], updated], axis=0)
    high, low = halves(state)
    u = mix(a_mid[2], [high, low, high], tiled(bu_mid[2], cells))
    u_out[...] = u
    latent = jnp.where(iota((16, cells), 0) < 12, u[:16], 0.0)
    total = total - 0.5 * jnp.sum(latent * latent, keepdims=True)
    sum_out[...] = jnp.broadcast_to(total, (8, 128))
    own = u_out[0:16, pl.ds(pl.multiple_of(where[0] * 256, 256), 256)]
    for j in range(8):
        latent_out[j] = own[:12, 32 * j : 32 * j + 32]


def top_kernel(u_in, sum_in, where, const, w1m, w2m, b2m, w3m, b3m, a_top0, a_top1, bu_top, w1, w2, b2, w3, b3,
               latent_out, sum_out, x_scr, p_scr, xt_scr, pt_scr):
    updated, logs = mid_update(u_in[...], 2, (w1m, w2m, b2m, w3m, b3m), x_scr, p_scr)
    total = sum_in[0:1, 0:1] + const[0:1, 0:1] + logs
    high, low = halves(updated)
    cell = iota((128, 128), 0)
    target = 32 * (2 * (cell // 32 % 2) + cell % 2) + 16 * (cell // 64) + cell % 32 // 2
    order = (target == iota((128, 128), 1)).astype(BF)
    stacked = jnp.concatenate([part[:, 128 * k : 128 * k + 128] for part in (high, low) for k in range(16)], axis=0)
    stacked = dot(stacked, order)
    lane = iota((16, 128), 1) // 32
    parts = []
    for p in range(2):
        for ij in range(4):
            pieces = []
            for m in range(4):
                piece = None
                for j in range(4):
                    start = 256 * p + 16 * (4 * m + j)
                    source = stacked[start : start + 16]
                    turn = (32 * (j - ij)) % 128
                    source = pltpu.roll(source, turn, 1) if turn else source
                    piece = source if piece is None else jnp.where(lane == j, source, piece)
                pieces.append(piece)
            parts.append(jnp.concatenate(pieces, axis=1).astype(BF))
    u = mix(a_top0[...], parts + parts[:4], tiled(bu_top[0], 512))
    ones = (iota((8, 512), 0) == 0).astype(F32)
    for s in range(2):
        out = conditioner(u[:24], ones, w1[s], w2[s], b2[s], w3[s], b3[s], xt_scr, pt_scr, 16, 512)
        scale, logs = gate_of(out[:24])
        total = total + jnp.sum(logs, keepdims=True)
        state = jnp.concatenate([u[:24], (u[24:] + out[24:]) * scale], axis=0)
        if s == 0:
            high, low = halves(state)
            u = mix(a_top1[...], [high, low, high], tiled(bu_top[1], 512))
    total = total - 0.5 * jnp.sum(state * state, keepdims=True)
    total = (total - 0.5 * log_two_pi * 49152.0) * (1.0 / 49152.0)
    sum_out[...] = jnp.broadcast_to(total, (8, 128))
    block = pltpu.roll(state, (512 - where[0] * 64) % 512, 1)
    latent_out[...] = block[:, :64]


def pack_kernel(images, packed):
    for i in range(8):
        rows = images[i]
        wide = jnp.concatenate([rows[0:8], rows[8:16], rows[16:24], jnp.zeros((8, 32), F32)], axis=1)
        for r in range(8):
            packed[8 * r + i] = wide


def shapes(*items):
    return tuple(jax.ShapeDtypeStruct(shape, dtype) for shape, dtype in items)


def body(images, *params):
    picked = pl.pallas_call(
        pack_kernel, in_specs=[VMEM], out_specs=VMEM, out_shape=jax.ShapeDtypeStruct((64, 8, 128), F32), name="pack"
    )(images.reshape(8, 24, 32))
    slots = lax.all_to_all(picked, ("rows", "chan"), 0, 0, tiled=True)
    prepared = pl.pallas_call(
        prep_kernel,
        in_specs=[VMEM] * 22,
        out_specs=(VMEM,) * 16,
        out_shape=shapes(
            ((3, 32, 96), BF), ((3, 32, 128), F32), ((3, 512, 144), BF), ((3, 512, 512), BF), ((3, 512, 128), F32),
            ((3, 216, 512), BF), ((3, 24, 128), F32),
            ((48, 192), BF), ((48, 144), BF), ((2, 48, 128), F32), ((2, 512, 224), BF), ((2, 512, 512), BF),
            ((2, 512, 128), F32), ((2, 432, 512), BF), ((2, 48, 128), F32), ((8, 128), F32),
        ),
        name="prep",
    )(*params)
    a_mid, bu_mid, *mid = prepared[:7]
    *top, const = prepared[7:]
    where = lax.axis_index("rows").astype(jnp.int32).reshape(1)
    u, sums, latent = pl.pallas_call(
        mid_kernel,
        in_specs=[VMEM, SMEM] + [VMEM] * 7,
        out_specs=(VMEM,) * 3,
        out_shape=shapes(((32, 2048), F32), ((8, 128), F32), ((8, 12, 32), F32)),
        scratch_shapes=[pltpu.VMEM((144, 2048), BF), pltpu.VMEM((216, 2048), F32)],
        name="mid",
    )(slots, where, a_mid, bu_mid, *mid)
    latent_mid = lax.all_to_all(latent, "chan", 0, 0, tiled=True)
    latent_top, loglik = pl.pallas_call(
        top_kernel,
        in_specs=[VMEM, VMEM, SMEM] + [VMEM] * 14,
        out_specs=(VMEM,) * 2,
        out_shape=shapes(((48, 64), F32), ((8, 128), F32)),
        scratch_shapes=[
            pltpu.VMEM((144, 2048), BF), pltpu.VMEM((216, 2048), F32), pltpu.VMEM((224, 512), BF), pltpu.VMEM((432, 512), F32),
        ],
        name="top",
    )(u, sums, where, const, *mid, *top)
    return latent_mid.reshape(8, 12, 1, 32), latent_top.reshape(1, 48, 4, 16), loglik[0, :1]


def solution(mesh):
    return jax.shard_map(
        body,
        mesh=mesh,
        in_specs=(P("batch", None, ("rows", "chan"), None),) + (P(),) * 22,
        out_specs=(
            P("batch", None, ("rows", "chan"), None),
            P(("batch", "chan"), None, "rows", None),
            P(("batch", "chan")),
        ),
        check_vma=False,
    )
```

time: 226 us -> 71.9 us (0.32); the launches traced: 222 us -> 71.4 us
  waiting for transfers between devices: 60.7 us -> 0.01 us
  starting transfers between devices: 84.2 us -> 25 us
  matrix products: 47.6 us -> 0 us
  Pallas kernels: 0 us -> 32.6 us
  between operations: 12.4 us -> 0.68 us
  other arithmetic: 11.4 us -> 0.68 us
  local copies, waits for them, and re-layouts: 5.92 us -> 12.4 us
    ppermute x20 -> x0, starting transfers between devices: 61.9 us -> none  [the longest x4 25 us: with_halo(): lax.ppermute(lax.slice_in_dim(block, block.shape[dim] - width, None, axis...]
    dot_general x100 -> x0, matrix products: 47.6 us -> none  [the longest x45 30.4 us: conv_out(): jnp.einsum('bhwc,co->bohw', window, weights[tap_idx], preferred_element_t...]
    ppermute x20 -> x0, waiting for transfers between devices: 41 us -> none  [the longest x6 34.4 us: padded_2(): lax.ppermute(first, axis, [(b, a) for a, b in up])]
    pallas_call x0 -> x4, Pallas kernels: none -> 32.6 us  [the longest x1 10.5 us: body(): pl.pallas_call(top_kernel, in_specs=[VMEM, VMEM, SMEM] + [VMEM] * 14, out...]
    all_to_all x3 -> x2, waiting for transfers between devices: 19.7 us -> 0.01 us  [the longest x1 0.01 us: body(): slots = lax.all_to_all(picked, ('rows', 'chan'), 0, 0, tiled=True)]
    unnamed x33 -> x9, local copies, waits for them, and re-layouts: 2.15 us -> 9.3 us
    reduce_sum x10 -> x0, other arithmetic: 6.51 us -> none  [the longest x2 2.19 us: flow_step(): jnp.sum(diag_log)]
    all_to_all x3 -> x2, starting transfers between devices: 22.3 us -> 25 us  [the longest x1 17.8 us: body(): slots = lax.all_to_all(picked, ('rows', 'chan'), 0, 0, tiled=True)]
  transfers between devices with their start and end apart: 23 -> 2, of which waited for: 13 -> 0; matrix products, arithmetic and copies ran while one was open for 3% -> 13% of each run, Pallas kernels for 0% -> 29%
where the time goes in v1:
time: 71.9 us; the launch traced here: 71.4 us
  Pallas kernels  32.6 us (45%)
  starting transfers between devices  25 us (35%)
  local copies, waits for them, and re-layouts  12.4 us (17%)
    all_to_all x1, starting transfers between devices, body(): slots = lax.all_to_all(picked, ('rows', 'chan'), 0, 0, tiled=True)  17.8 us
    pallas_call x1, Pallas kernels, body(): pl.pallas_call(top_kernel, in_specs=[VMEM, VMEM, SMEM] + [VMEM] * 14, out...  10.5 us
    pallas_call x1, Pallas kernels, body(): pl.pallas_call(prep_kernel, in_specs=[VMEM] * 22, out_specs=(VMEM,) * 16,...  10.5 us
    pallas_call x1, Pallas kernels, body(): pl.pallas_call(mid_kernel, in_specs=[VMEM, SMEM] + [VMEM] * 7, out_specs=...  9.96 us
    unnamed x9, local copies, waits for them, and re-layouts  9.3 us
    all_to_all x1, starting transfers between devices, body(): latent_mid = lax.all_to_all(latent, 'chan', 0, 0, tiled=True)  7.21 us
    pallas_call x1, Pallas kernels, body(): pl.pallas_call(pack_kernel, in_specs=[VMEM], out_specs=VMEM, out_shape=ja...  1.7 us
  transfers between devices with their start and end apart: 2, of which 0 were waited for; matrix products, arithmetic and copies ran while one was open for 13% of the time, Pallas kernels for 29%

profile of v1, /device:TPU:1, one launch (start us, length us, event | category | flops | bytes accessed | tf_op | source)
XLA Modules:
  0.0 71.4 jit_solution(2402681282951899739)
XLA Ops:
  0.6 1.7 %pack.1 = f32[64,8,128]{2,1,0:T(8,128)} custom-call(f32[8,24,32]{2,1,0:T(8,128)} %bitcast.6), custom_call_target="tpu_custom_call" | custom-call | tf_op jit(solution)/shard_map/pack/pallas_call | solution.py:295
  2.3 0.0 copy-start.1
  2.3 17.8 %all-to-all-start = ((f32[64,8,128]{2,1,0:T(8,128)}), f32[64,8,128]{2,1,0:T(8,128)S(1)}, u32[]{:S(2)}, u32[]{:S(2)}) async-start(f32[64,8,128]{2,1,0:T(8,128)} %pack.1), calls=%async_computation | async-start | bytes 524288 | tf_op jit(solution)/shard_map/all_to_all | solution.py:298
  20.1 3.9 %copy.30.third_mid = bf16[3,9,512,24]{3,2,1,0:T(8,128)(2,1)} copy(bf16[3,9,512,24]{2,3,1,0:T(8,128)(2,1)} %param.33) | data formatting | bytes 1327104 | tf_op args[10]
  24.0 0.0 copy-done.1
  24.0 2.4 %copy.31.third_top = bf16[2,9,512,48]{3,2,1,0:T(8,128)(2,1)} copy(bf16[2,9,512,48]{2,3,1,0:T(8,128)(2,1)S(1)} %copy-done.1) | data formatting | bytes 1769472 | tf_op args[21]
  26.4 10.5 %prep.1 = (bf16[3,32,96]{2,1,0:T(8,128)(2,1)}, f32[3,32,128]{2,1,0:T(8,128)}, bf16[3,512,144]{2,1,0:T(8,128)(2,1)}, bf16[3,512,512]{2,1,0:T(8,128)(2,1)}, f32[3,...) custom-call(f32[3,24]{1,0:T(4,128)} %shift_mid.1, ...), custom_call_target="tpu_custom_call" | custom-call | tf_op jit(solution)/shard_map/prep/pallas_call | solution.py:299
  36.9 0.0 all-to-all-done.slots
  36.9 0.0 copy-start
  36.9 0.7 copy-done
  37.6 10.0 %mid.1 = (f32[32,2048]{1,0:T(8,128)}, f32[8,128]{1,0:T(8,128)}, f32[8,12,32]{2,1,0:T(8,128)}) custom-call(f32[64,8,128]{2,1,0:T(8,128)} %copy-done, s32[1]{0:T(128)} %bitcast.1.where, bf16[3,32,96]{2,1,0:T(8,128)(2,1)} %get-tuple-element.24.a_mid, f32[3,32,128]{2,1,0:T(8,128)} %get-tuple-element.25.bu_mid, bf16[3,512,144]{2,1,0:T(8,128)(2,1)} %get-tuple-element.26.w1.w1m, ...), custom_call_target="tpu_custom_call" | custom-call | tf_op jit(solution)/shard_map/mid/pallas_call | solution.py:314
  47.6 1.5 %reshape.22 = f32[8,1,384]{2,1,0:T(1,128)} reshape(f32[8,12,32]{2,1,0:T(8,128)} %get-tuple-element.31) | data formatting | bytes 24576
  49.1 7.2 %all-to-all-start.1 = ((f32[8,1,384]{2,1,0:T(1,128)}), f32[8,1,384]{2,1,0:T(1,128)S(1)}, u32[]{:S(2)}, u32[]{:S(2)}) async-start(f32[8,1,384]{2,1,0:T(1,128)} %reshape.22), calls=%async_computation.1 | async-start | bytes 24576 | tf_op jit(solution)/shard_map/all_to_all | solution.py:322
  56.3 10.5 %top.1 = (f32[48,64]{1,0:T(8,128)}, f32[8,128]{1,0:T(8,128)}) custom-call(f32[32,2048]{1,0:T(8,128)} %get-tuple-element.32.u_in, f32[8,128]{1,0:T(8,128)} %get-tuple-element.33.sum_in, s32[1]{0:T(128)} %bitcast.1.where, f32[8,128]{1,0:T(8,128)} %get-tuple-element.34.const, bf16[3,512,144]{2,1,0:T(8,128)(2,1)} %get-tuple-element.26.w1.w1m, ...), custom_call_target="tpu_custom_call" | custom-call | tf_op jit(solution)/shard_map/top/pallas_call | solution.py:323
  66.8 1.4 %copy.32 = f32[48,64]{0,1:T(8,128)} copy(f32[48,64]{1,0:T(8,128)} %get-tuple-element.43) | data formatting | bytes 24576 | tf_op jit(solution)/shard_map/top/pallas_call | solution.py:323
  68.3 1.2 %slice.3 = f32[1,1]{1,0:T(1,128)} slice(f32[8,128]{1,0:T(8,128)} %get-tuple-element.44), slice={[0:1], [0:1]} | slice | bytes 8 | tf_op jit(solution)/shard_map/slice | solution.py:333
  69.5 0.0 all-to-all-done.1
  69.5 0.5 broadcast
  70.0 0.7 reduce
  70.7 0.1 reshape.23
  70.7 0.7 copy.33
Async XLA Ops:
  2.3 21.7 %copy-start.1 = (bf16[2,9,512,48]{2,3,1,0:T(8,128)(2,1)S(1)}, bf16[2,9,512,48]{2,3,1,0:T(8,128)(2,1)}, u32[]{:S(2)}) copy-start(bf16[2,9,512,48]{2,3,1,0:T(8,128)(2,1)} %param.44) | copy-start | bytes 2654212
  2.3 34.6 %all-to-all-start = ((f32[64,8,128]{2,1,0:T(8,128)}), f32[64,8,128]{2,1,0:T(8,128)S(1)}, u32[]{:S(2)}, u32[]{:S(2)}) async-start(f32[64,8,128]{2,1,0:T(8,128)} %pack.1), calls=%async_computation | async-start | bytes 524288 | tf_op jit(solution)/shard_map/all_to_all | solution.py:298
  36.9 0.7 copy-start
  49.1 20.4 %all-to-all-start.1 = ((f32[8,1,384]{2,1,0:T(1,128)}), f32[8,1,384]{2,1,0:T(1,128)S(1)}, u32[]{:S(2)}, u32[]{:S(2)}) async-start(f32[8,1,384]{2,1,0:T(1,128)} %reshape.22), calls=%async_computation.1 | async-start | bytes 24576 | tf_op jit(solution)/shard_map/all_to_all | solution.py:322

commit v2 on v1

--- a/solution.py
+++ b/solution.py
@@ -13,6 +13,7 @@
 log_two_pi = math.log(2.0 * math.pi)
 VMEM = pl.BlockSpec(memory_space=pltpu.VMEM)
 SMEM = pl.BlockSpec(memory_space=pltpu.SMEM)
+HBM = pl.BlockSpec(memory_space=pltpu.HBM)
 
 
 def iota(shape, dim):
@@ -70,11 +71,11 @@
 
 def prep_kernel(
     shift_mid, gain_mid, lower_mid, upper_mid, diag_mid, first_mid, first_bias_mid, second_mid,
-    second_bias_mid, third_mid, third_bias_mid,
+    second_bias_mid, third_bias_mid,
     shift_top, gain_top, lower_top, upper_top, diag_top, first_top, first_bias_top, second_top,
-    second_bias_top, third_top, third_bias_top,
-    a_mid, bu_mid, w1_mid, w2_mid, b2_mid, w3_mid, b3_mid,
-    a_top0, a_top1, bu_top, w1_top, w2_top, b2_top, w3_top, b3_top, const,
+    second_bias_top, third_bias_top,
+    a_mid, bu_mid, w1_mid, w2_mid, b2_mid, b3_mid,
+    a_top0, a_top1, bu_top, w1_top, w2_top, b2_top, b3_top, const,
 ):
     hid = second_mid.shape[1]
     ident = eye(hid, BF)
@@ -100,9 +101,7 @@
             blocks += [first_mid[s, tap].astype(F32), with_bias if tap == 4 else zeros]
         w1_mid[s] = dot_t(ident, jnp.concatenate(blocks, axis=0).astype(BF)).astype(BF)
         w2_mid[s] = dot_t(ident, second_mid[s]).astype(BF)
-        b2_mid[s] = jnp.broadcast_to(second_bias_mid[row], (128, hid)).T
-        for tap in range(9):
-            w3_mid[s, 24 * tap : 24 * tap + 24, :] = dot_t(eye(24, BF), third_mid[s, tap]).astype(BF)
+        b2_mid[s] = jnp.broadcast_to(second_bias_mid[row], (8, hid))
         b3 = to_column(third_bias_mid[row]) + jnp.where(iota((24, 1), 0) < 12, 2.0, 0.0)
         b3_mid[s] = jnp.broadcast_to(b3, (24, 128))
     for s in range(2):
@@ -121,8 +120,6 @@
         w1_top[s] = dot_t(ident, jnp.concatenate(blocks, axis=0).astype(BF)).astype(BF)
         w2_top[s] = dot_t(ident, second_top[s]).astype(BF)
         b2_top[s] = jnp.broadcast_to(second_bias_top[row], (128, hid)).T
-        for tap in range(9):
-            w3_top[s, 48 * tap : 48 * tap + 48, :] = dot_t(eye(48, BF), third_top[s, tap]).astype(BF)
         b3 = to_column(third_bias_top[row]) + jnp.where(iota((48, 1), 0) < 24, 2.0, 0.0)
         b3_top[s] = jnp.broadcast_to(b3, (48, 128))
     const[...] = jnp.broadcast_to(total, (8, 128))
@@ -153,7 +150,7 @@
     return jnp.where(inside, moved(x, dc), 0.0)
 
 
-def conditioner(q, extra, w1, w2, b2, w3, b3, x_scr, p_scr, width, chunk):
+def conditioner(q, extra, refs, copies, x_scr, p_scr, width, chunk):
     cells = q.shape[1]
     rows = q.shape[0]
     sides = [column_moved(q, dc, width) for dc in (-1, 0, 1)]
@@ -161,13 +158,22 @@
     if extra is not None:
         blocks.append(extra)
     x_scr[...] = jnp.concatenate(blocks, axis=0).astype(BF)
+    if len(copies) > 1:
+        awaited(copies)
+    w1_ref, w2_ref, b2_ref, w3_ref, b3_ref = refs
+    w1, w2, b3 = w1_ref[...], w2_ref[...], b3_ref[...]
+    b2 = b2_ref[...]
+    if b2.shape[0] == 8:
+        b2 = jnp.concatenate([b2] * 16, axis=0).T
     bias = tiled(b2, chunk)
 
     def one(i):
         at = pl.ds(i * chunk, chunk)
         inner = jnp.maximum(dot(w1, x_scr[:, at]), 0.0).astype(BF)
         middle = jnp.maximum(dot(w2, inner) + bias, 0.0).astype(BF)
-        p_scr[:, at] = dot(w3, middle)
+        if i == 0 and len(copies) == 1:
+            awaited(copies)
+        p_scr[:, at] = dot(w3_ref[...], middle)
 
     for i in range(cells // chunk):
         one(i)
@@ -193,17 +199,28 @@
     return dot(a, jnp.concatenate(parts, axis=0)) + bias
 
 
-def mid_update(u, s, refs, x_scr, p_scr):
-    w1, w2, b2, w3, b3 = refs
-    out = conditioner(u[:16], None, w1[s], w2[s], b2[s], w3[s], b3[s], x_scr, p_scr, 32, 512)
+def mid_update(u, refs, copies, x_scr, p_scr):
+    out = conditioner(u[:16], None, refs, copies, x_scr, p_scr, 32, 1024)
     scale, logs = gate_of(out[:16])
     logs = jnp.where(iota(logs.shape, 0) < 12, logs, 0.0)
     updated = (u[16:] + out[8:]) * pltpu.roll(scale, 4, 0)
     return updated, jnp.sum(logs, keepdims=True)
 
 
-def mid_kernel(slots, where, a_mid, bu_mid, w1, w2, b2, w3, b3, u_out, sum_out, latent_out, x_scr, p_scr):
-    refs = (w1, w2, b2, w3, b3)
+def started(pairs, sems):
+    copies = [pltpu.make_async_copy(a, b, sems.at[k]) for k, (a, b) in enumerate(pairs)]
+    for copy in copies:
+        copy.start()
+    return copies
+
+
+def awaited(copies):
+    for copy in copies:
+        copy.wait()
+
+
+def mid_kernel(where, slots, a_mid, bu_mid, b3, w1, w2, b2, w3h, u_out, sum_out, latent_out, x_scr, p_scr, w3, sems):
+    copies = started([(w3h.at[s], w3.at[s]) for s in range(2)], sems)
     cells = 2048
     lane = iota((8, 128), 1) // 32
     groups = []
@@ -223,7 +240,7 @@
     for s in range(2):
         high, low = halves(state)
         u = mix(a_mid[s], [high, low, high], tiled(bu_mid[s], cells))
-        updated, logs = mid_update(u, s, refs, x_scr, p_scr)
+        updated, logs = mid_update(u, (w1.at[s], w2.at[s], b2.at[s], w3.at[s], b3.at[s]), copies[s : s + 1], x_scr, p_scr)
         total = total + logs
         state = jnp.concatenate([u[:16], updated], axis=0)
     high, low = halves(state)
@@ -234,12 +251,20 @@
     sum_out[...] = jnp.broadcast_to(total, (8, 128))
     own = u_out[0:16, pl.ds(pl.multiple_of(where[0] * 256, 256), 256)]
     for j in range(8):
-        latent_out[j] = own[:12, 32 * j : 32 * j + 32]
-
-
-def top_kernel(u_in, sum_in, where, const, w1m, w2m, b2m, w3m, b3m, a_top0, a_top1, bu_top, w1, w2, b2, w3, b3,
-               latent_out, sum_out, x_scr, p_scr, xt_scr, pt_scr):
-    updated, logs = mid_update(u_in[...], 2, (w1m, w2m, b2m, w3m, b3m), x_scr, p_scr)
+        part = own[:, 128 * (j // 4) : 128 * (j // 4) + 128]
+        latent_out[j] = pltpu.roll(part, 128 - 32 * (j % 4), 1) if j % 4 else part
+
+
+def top_kernel(where, u_in, sum_in, b3m, w1m, w2m, b2m, w3mh, w1h, w2h, b2h, w3h, *rest):
+    small_h, (latent_out, sum_out, x_scr, p_scr, xt_scr, pt_scr, w3m, w1, w2, b2, w3, *small, sems) = rest[:5], rest[5:]
+    a_top0, a_top1, bu_top, b3, const = small
+    pairs = [(w3mh.at[2], w3m)] + list(zip(small_h, small))
+    for s in range(2):
+        pairs += [(a.at[s], b.at[s]) for a, b in zip((w1h, w2h, b2h, w3h), (w1, w2, b2, w3))]
+    copies = started(pairs, sems)
+    refs = (w1m.at[2], w2m.at[2], b2m.at[2], w3m, b3m.at[2])
+    updated, logs = mid_update(u_in[...], refs, copies[:1], x_scr, p_scr)
+    awaited(copies[1:6])
     total = sum_in[0:1, 0:1] + const[0:1, 0:1] + logs
     high, low = halves(updated)
     cell = iota((128, 128), 0)
@@ -265,7 +290,7 @@
     u = mix(a_top0[...], parts + parts[:4], tiled(bu_top[0], 512))
     ones = (iota((8, 512), 0) == 0).astype(F32)
     for s in range(2):
-        out = conditioner(u[:24], ones, w1[s], w2[s], b2[s], w3[s], b3[s], xt_scr, pt_scr, 16, 512)
+        out = conditioner(u[:24], ones, (w1.at[s], w2.at[s], b2.at[s], w3.at[s], b3.at[s]), copies[6 + 4 * s : 10 + 4 * s], xt_scr, pt_scr, 16, 512)
         scale, logs = gate_of(out[:24])
         total = total + jnp.sum(logs, keepdims=True)
         state = jnp.concatenate([u[:24], (u[24:] + out[24:]) * scale], axis=0)
@@ -274,9 +299,10 @@
             u = mix(a_top1[...], [high, low, high], tiled(bu_top[1], 512))
     total = total - 0.5 * jnp.sum(state * state, keepdims=True)
     total = (total - 0.5 * log_two_pi * 49152.0) * (1.0 / 49152.0)
-    sum_out[...] = jnp.broadcast_to(total, (8, 128))
+    sum_out[0] = total[0, 0]
     block = pltpu.roll(state, (512 - where[0] * 64) % 512, 1)
-    latent_out[...] = block[:, :64]
+    block = jnp.concatenate([block[:, :128], jnp.zeros((80, 128), F32)], axis=0)
+    latent_out[...] = block.T[:64, :48]
 
 
 def pack_kernel(images, packed):
@@ -291,46 +317,99 @@
     return tuple(jax.ShapeDtypeStruct(shape, dtype) for shape, dtype in items)
 
 
-def body(images, *params):
-    picked = pl.pallas_call(
+def in_vmem(x):
+    return pltpu.with_memory_space_constraint(x, pltpu.VMEM)
+
+
+def in_hbm(x):
+    return pltpu.with_memory_space_constraint(x, pltpu.HBM)
+
+
+def call(kernel, name, inputs, specs, outputs, scratch=(), out_specs=None, limit=None):
+    return pl.pallas_call(
+        kernel,
+        in_specs=specs,
+        out_specs=out_specs or (VMEM,) * len(outputs),
+        out_shape=tuple(outputs),
+        scratch_shapes=list(scratch),
+        compiler_params=pltpu.CompilerParams(vmem_limit_bytes=limit),
+        name=name,
+    )(*inputs)
+
+
+def pack(images):
+    return pl.pallas_call(
         pack_kernel, in_specs=[VMEM], out_specs=VMEM, out_shape=jax.ShapeDtypeStruct((64, 8, 128), F32), name="pack"
     )(images.reshape(8, 24, 32))
-    slots = lax.all_to_all(picked, ("rows", "chan"), 0, 0, tiled=True)
-    prepared = pl.pallas_call(
+
+
+def prep(params):
+    small = [p for i, p in enumerate(params) if i not in (9, 20)]
+    return call(
         prep_kernel,
-        in_specs=[VMEM] * 22,
-        out_specs=(VMEM,) * 16,
-        out_shape=shapes(
-            ((3, 32, 96), BF), ((3, 32, 128), F32), ((3, 512, 144), BF), ((3, 512, 512), BF), ((3, 512, 128), F32),
-            ((3, 216, 512), BF), ((3, 24, 128), F32),
-            ((48, 192), BF), ((48, 144), BF), ((2, 48, 128), F32), ((2, 512, 224), BF), ((2, 512, 512), BF),
-            ((2, 512, 128), F32), ((2, 432, 512), BF), ((2, 48, 128), F32), ((8, 128), F32),
+        "prep",
+        small,
+        [VMEM] * 20,
+        (
+            pltpu.VMEM((3, 32, 96), BF), pltpu.VMEM((3, 32, 128), F32), pltpu.VMEM((3, 512, 144), BF), pltpu.VMEM((3, 512, 512), BF),
+            pltpu.VMEM((3, 8, 512), F32), pltpu.VMEM((3, 24, 128), F32),
+        )
+        + shapes(
+            ((48, 192), BF), ((48, 144), BF), ((2, 48, 128), F32), ((2, 512, 224), BF), ((2, 512, 512), BF), ((2, 512, 128), F32),
+            ((2, 48, 128), F32), ((8, 128), F32),
         ),
-        name="prep",
-    )(*params)
-    a_mid, bu_mid, *mid = prepared[:7]
-    *top, const = prepared[7:]
+    )
+
+
+MID_SCRATCH = (pltpu.VMEM((144, 2048), BF), pltpu.VMEM((216, 2048), F32))
+
+
+def mid(where, slots, prepared, third):
+    a, bu, w1, w2, b2, b3 = (in_vmem(x) for x in prepared[:6])
+    return call(
+        mid_kernel,
+        "mid",
+        [where, in_vmem(slots), a, bu, b3, w1, w2, b2, in_hbm(third)],
+        [SMEM] + [VMEM] * 7 + [HBM],
+        [pltpu.VMEM((32, 2048), F32), pltpu.VMEM((8, 128), F32), jax.ShapeDtypeStruct((8, 16, 128), F32)],
+        MID_SCRATCH + (pltpu.VMEM((2, 216, 512), BF), pltpu.SemaphoreType.DMA((2,))),
+        limit=24 * 2**20,
+    )
+
+
+def top(where, u, sums, prepared, third_m, third):
+    w1m, w2m, b2m, b3m = (in_vmem(x) for x in prepared[2:6])
+    a0, a1, bu, w1, w2, b2, b3, const = prepared[6:]
+    return call(
+        top_kernel,
+        "top",
+        [where, in_vmem(u), in_vmem(sums), b3m, w1m, w2m, b2m]
+        + [in_hbm(x) for x in (third_m, w1, w2, b2, third, a0, a1, bu, b3, const)],
+        [SMEM] + [VMEM] * 6 + [HBM] * 10,
+        [jax.ShapeDtypeStruct((64, 48), F32), jax.ShapeDtypeStruct((1,), F32)],
+        MID_SCRATCH
+        + (
+            pltpu.VMEM((224, 512), BF), pltpu.VMEM((432, 512), F32), pltpu.VMEM((216, 512), BF),
+            pltpu.VMEM((2, 512, 224), BF), pltpu.VMEM((2, 512, 512), BF), pltpu.VMEM((2, 512, 128), F32), pltpu.VMEM((2, 432, 512), BF),
+            pltpu.VMEM((48, 192), BF), pltpu.VMEM((48, 144), BF), pltpu.VMEM((2, 48, 128), F32), pltpu.VMEM((2, 48, 128), F32), pltpu.VMEM((8, 128), F32),
+            pltpu.SemaphoreType.DMA((14,)),
+        ),
+        (VMEM, SMEM),
+        limit=24 * 2**20,
+    )
+
+
+def body(images, *params):
+    slots = lax.all_to_all(pack(images), ("rows", "chan"), 0, 0, tiled=True)
+    third_mid = params[9].transpose(0, 1, 3, 2).reshape(3, 216, 512)
+    third_top = params[20].transpose(0, 1, 3, 2).reshape(2, 432, 512)
+    prepared = prep(params)
     where = lax.axis_index("rows").astype(jnp.int32).reshape(1)
-    u, sums, latent = pl.pallas_call(
-        mid_kernel,
-        in_specs=[VMEM, SMEM] + [VMEM] * 7,
-        out_specs=(VMEM,) * 3,
-        out_shape=shapes(((32, 2048), F32), ((8, 128), F32), ((8, 12, 32), F32)),
-        scratch_shapes=[pltpu.VMEM((144, 2048), BF), pltpu.VMEM((216, 2048), F32)],
-        name="mid",
-    )(slots, where, a_mid, bu_mid, *mid)
+    u, sums, latent = mid(where, slots, prepared, third_mid)
     latent_mid = lax.all_to_all(latent, "chan", 0, 0, tiled=True)
-    latent_top, loglik = pl.pallas_call(
-        top_kernel,
-        in_specs=[VMEM, VMEM, SMEM] + [VMEM] * 14,
-        out_specs=(VMEM,) * 2,
-        out_shape=shapes(((48, 64), F32), ((8, 128), F32)),
-        scratch_shapes=[
-            pltpu.VMEM((144, 2048), BF), pltpu.VMEM((216, 2048), F32), pltpu.VMEM((224, 512), BF), pltpu.VMEM((432, 512), F32),
-        ],
-        name="top",
-    )(u, sums, where, const, *mid, *top)
-    return latent_mid.reshape(8, 12, 1, 32), latent_top.reshape(1, 48, 4, 16), loglik[0, :1]
+    latent_top, loglik = top(where, u, sums, prepared, third_mid, third_top)
+    latent_top = latent_top.reshape(1, 4, 16, 48).transpose(0, 3, 1, 2)
+    return latent_mid[:, :12, None, :32], latent_top, loglik
 
 
 def solution(mesh):

time: 71.9 us -> 55.6 us (0.77)
  local copies, waits for them, and re-layouts: 12.4 us -> 0.68 us
  Pallas kernels: 32.6 us -> 23.6 us
  waiting for transfers between devices: 0.01 us -> 8.84 us
  starting transfers between devices: 25 us -> 21.5 us
    pallas_call x4, Pallas kernels: 32.6 us -> 23.6 us  [the longest x3 21.9 us: call(): pl.pallas_call(kernel, in_specs=specs, out_specs=out_specs or (VMEM,) * l...]
    all_to_all x1, waiting for transfers between devices: 0.01 us -> 8.83 us  [body(): slots = lax.all_to_all(pack(images), ('rows', 'chan'), 0, 0, tiled=True)]
    unnamed x9 -> x1, local copies, waits for them, and re-layouts: 9.3 us -> 0.67 us
    all_to_all x1, starting transfers between devices: 7.21 us -> 3.91 us  [body(): latent_mid = lax.all_to_all(latent, 'chan', 0, 0, tiled=True)]
    pallas_call x1 -> x0, local copies, waits for them, and re-layouts: 1.43 us -> none  [body(): pl.pallas_call(top_kernel, in_specs=[VMEM, VMEM, SMEM] + [VMEM] * 14, out...]
    slice x1 -> x0, local copies, waits for them, and re-layouts: 1.18 us -> none  [body(): loglik[0, :1]]
  transfers between devices with their start and end apart: 2 -> 2, of which waited for: 0 -> 1; matrix products, arithmetic and copies ran while one was open for 13% -> 0% of each run, Pallas kernels for 29% -> 27%
where the time goes in v2:
time: 55.6 us; the launch traced here: 55.3 us
  Pallas kernels  23.6 us (42%)
  starting transfers between devices  21.5 us (39%)
  waiting for transfers between devices  8.84 us (16%)
  local copies, waits for them, and re-layouts  0.68 us (1%)
  between operations  0.68 us (1%)
    pallas_call x3, Pallas kernels, call(): pl.pallas_call(kernel, in_specs=specs, out_specs=out_specs or (VMEM,) * l...  21.9 us
    all_to_all x1, starting transfers between devices, body(): slots = lax.all_to_all(pack(images), ('rows', 'chan'), 0, 0, tiled=True)  17.6 us
    all_to_all x1, waiting for transfers between devices, body(): slots = lax.all_to_all(pack(images), ('rows', 'chan'), 0, 0, tiled=True)  8.83 us
    all_to_all x1, starting transfers between devices, body(): latent_mid = lax.all_to_all(latent, 'chan', 0, 0, tiled=True)  3.91 us
    pallas_call x1, Pallas kernels, pack(): pl.pallas_call(pack_kernel, in_specs=[VMEM], out_specs=VMEM, out_shape=ja...  1.69 us
  transfers between devices with their start and end apart: 2, of which 1 were waited for; matrix products, arithmetic and copies ran while one was open for 0% of the time, Pallas kernels for 27%

profile of v2, /device:TPU:1, one launch (start us, length us, event | category | flops | bytes accessed | tf_op | source)
XLA Modules:
  0.0 55.3 jit_solution(11433905725792747137)
XLA Ops:
  0.6 1.7 %pack.1 = f32[64,8,128]{2,1,0:T(8,128)} custom-call(f32[8,24,32]{2,1,0:T(8,128)} %bitcast.16), custom_call_target="tpu_custom_call" | custom-call | tf_op jit(solution)/shard_map/pack/pallas_call | solution.py:341
  2.3 17.6 %all-to-all-start = ((f32[64,8,128]{2,1,0:T(8,128)}), f32[64,8,128]{2,1,0:T(8,128)S(1)}, u32[]{:S(2)}, u32[]{:S(2)}) async-start(f32[64,8,128]{2,1,0:T(8,128)} %pack.1), calls=%async_computation | async-start | bytes 524288 | tf_op jit(solution)/shard_map/all_to_all | solution.py:403
  20.0 6.5 %prep.1 = (bf16[3,32,96]{2,1,0:T(8,128)(2,1)S(1)}, f32[3,32,128]{2,1,0:T(8,128)S(1)}, bf16[3,512,144]{2,1,0:T(8,128)(2,1)S(1)}, bf16[3,512,512]{2,1,0:T(8,128)(2...) custom-call(f32[3,24]{1,0:T(4,128)} %shift_mid.1, ...), custom_call_target="tpu_custom_call" | custom-call | tf_op jit(solution)/shard_map/prep/pallas_call | solution.py:329
  26.4 8.8 %all-to-all-done.slots = f32[64,8,128]{2,1,0:T(8,128)S(1)} async-done(((f32[64,8,128]{2,1,0:T(8,128)}), f32[64,8,128]{2,1,0:T(8,128)S(1)}, u32[]{:S(2)}, u32[]{:S(2)}) %all-to-all-start) | async-done | bytes 262176 | tf_op jit(solution)/shard_map/all_to_all | solution.py:403
  35.2 6.9 %mid.1 = (f32[32,2048]{1,0:T(8,128)S(1)}, f32[8,128]{1,0:T(8,128)S(1)}, f32[8,16,128]{2,1,0:T(8,128)}) custom-call(s32[1]{0:T(128)} %bitcast.where, f32[64,8,128]{2,1,0:T(8,128)S(1)} %all-to-all-done.slots, bf16[3,32,96]{2,1,0:T(8,128)(2,1)S(1)} %get-tuple-element.22.a_mid, f32[3,32,128]{2,1,0:T(8,128)S(1)} %get-tuple-element.23.bu_mid, ...), custom_call_target="tpu_custom_call" | custom-call | tf_op jit(solution)/shard_map/mid/pallas_call | solution.py:329
  42.2 3.9 %all-to-all-start.1 = ((f32[8,16,128]{2,1,0:T(8,128)}), f32[8,16,128]{2,1,0:T(8,128)S(1)}, u32[]{:S(2)}, u32[]{:S(2)}) async-start(f32[8,16,128]{2,1,0:T(8,128)} %get-tuple-element.28), calls=%async_computation.1 | async-start | bytes 131072 | tf_op jit(solution)/shard_map/all_to_all | solution.py:409
  46.1 8.5 %top.1 = (f32[64,48]{1,0:T(8,128)}, f32[1]{0:T(128)}) custom-call(s32[1]{0:T(128)} %bitcast.where, f32[32,2048]{1,0:T(8,128)S(1)} %get-tuple-element.29.u_in, f32[8,128]{1,0:T(8,128)S(1)} %get-tuple-element.30.sum_in, f32[3,24,128]{2,1,0:T(8,128)S(1)} %get-tuple-element.24.b3.b3m, bf16[3,512,144]{2,1,0:T(8,128)(2,1)S(1)} %get-tuple-element.25.w1.w1m, ...), custom_call_target="tpu_custom_call" | custom-call | tf_op jit(solution)/shard_map/top/pallas_call | solution.py:329
  54.6 0.0 all-to-all-done.1
  54.6 0.7 %copy.26 = f32[8,12,1,32]{3,2,1,0:T(1,128)} copy(f32[8,12,1,32]{3,1,0,2:T(8,128)S(1)} %slice_bitcast_fusion) | data formatting | bytes 24576
  (1 shorter events, 0.0 us)
Async XLA Ops:
  2.3 32.9 %all-to-all-start = ((f32[64,8,128]{2,1,0:T(8,128)}), f32[64,8,128]{2,1,0:T(8,128)S(1)}, u32[]{:S(2)}, u32[]{:S(2)}) async-start(f32[64,8,128]{2,1,0:T(8,128)} %pack.1), calls=%async_computation | async-start | bytes 524288 | tf_op jit(solution)/shard_map/all_to_all | solution.py:403
  42.2 12.4 %all-to-all-start.1 = ((f32[8,16,128]{2,1,0:T(8,128)}), f32[8,16,128]{2,1,0:T(8,128)S(1)}, u32[]{:S(2)}, u32[]{:S(2)}) async-start(f32[8,16,128]{2,1,0:T(8,128)} %get-tuple-element.28), calls=%async_computation.1 | async-start | bytes 131072 | tf_op jit(solution)/shard_map/all_to_all | solution.py:409

commit v3 on v2

--- a/solution.py
+++ b/solution.py
@@ -89,7 +89,8 @@
         offset = jnp.sum(rows * jnp.sum(jnp.where(eye(24, F32) > 0, offset, 0.0), axis=0, keepdims=True), axis=1, keepdims=True)
         offset = offset + (iota((32, 1), 0) == 12).astype(F32)
         if s == 0:
-            columns = (iota((24, 32), 0) == iota((24, 32), 1)).astype(F32)
+            held = iota((24, 32), 1)
+            columns = (iota((24, 32), 0) == jnp.where(held % 8 < 6, held // 8 * 6 + held % 8, -1)).astype(F32)
         else:
             columns = (iota((24, 32), 0) == spread_mid(iota((24, 32), 1))).astype(F32)
         a_mid[s] = three_term_left(exact_dot(matrix, columns))
@@ -157,7 +158,8 @@
     blocks = [row_moved(side, dr, width) for dr in (-1, 0, 1) for side in sides]
     if extra is not None:
         blocks.append(extra)
-    x_scr[...] = jnp.concatenate(blocks, axis=0).astype(BF)
+    x = jnp.concatenate(blocks, axis=0).astype(BF)
+    outs = []
     if len(copies) > 1:
         awaited(copies)
     w1_ref, w2_ref, b2_ref, w3_ref, b3_ref = refs
@@ -167,23 +169,20 @@
         b2 = jnp.concatenate([b2] * 16, axis=0).T
     bias = tiled(b2, chunk)
 
-    def one(i):
-        at = pl.ds(i * chunk, chunk)
-        inner = jnp.maximum(dot(w1, x_scr[:, at]), 0.0).astype(BF)
-        middle = jnp.maximum(dot(w2, inner) + bias, 0.0).astype(BF)
-        if i == 0 and len(copies) == 1:
-            awaited(copies)
-        p_scr[:, at] = dot(w3_ref[...], middle)
-
-    for i in range(cells // chunk):
-        one(i)
-    n_out = p_scr.shape[0] // 9
+    n = cells // chunk
+    inner = [jnp.maximum(dot(w1, x[:, i * chunk : (i + 1) * chunk]), 0.0).astype(BF) for i in range(n)]
+    middle = [jnp.maximum(dot(w2, y) + bias, 0.0).astype(BF) for y in inner]
+    if len(copies) == 1:
+        awaited(copies)
+    outs = [dot(w3_ref[...], y) for y in middle]
+    p = outs[0] if len(outs) == 1 else jnp.concatenate(outs, axis=1)
+    n_out = p.shape[0] // 9
     out = tiled(b3, cells)
     for dc in (-1, 0, 1):
         part = None
         for dr in (-1, 0, 1):
             tap = 3 * (dr + 1) + dc + 1
-            term = row_moved(p_scr[n_out * tap : n_out * (tap + 1), :], dr, width)
+            term = row_moved(p[n_out * tap : n_out * (tap + 1), :], dr, width)
             part = term if part is None else part + term
         out = out + column_moved(part, dc, width)
     return out
@@ -199,8 +198,8 @@
     return dot(a, jnp.concatenate(parts, axis=0)) + bias
 
 
-def mid_update(u, refs, copies, x_scr, p_scr):
-    out = conditioner(u[:16], None, refs, copies, x_scr, p_scr, 32, 1024)
+def mid_update(u, refs, copies, x_scr, p_scr, chunk=1024):
+    out = conditioner(u[:16], None, refs, copies, x_scr, p_scr, 32, chunk)
     scale, logs = gate_of(out[:16])
     logs = jnp.where(iota(logs.shape, 0) < 12, logs, 0.0)
     updated = (u[16:] + out[8:]) * pltpu.roll(scale, 4, 0)
@@ -224,18 +223,18 @@
     cells = 2048
     lane = iota((8, 128), 1) // 32
     groups = []
-    for g in range(3):
+    for g in range(4):
         pieces = []
         for k in range(16):
             piece = None
             for j in range(4):
-                source = slots[4 * k + j]
+                source = jnp.concatenate([slots[4 * k + j, t] for t in range(3)] + [jnp.zeros((2, 128), F32)], axis=0)
                 turn = (32 * (j - g)) % 128
                 source = pltpu.roll(source, turn, 1) if turn else source
                 piece = source if piece is None else jnp.where(lane == j, source, piece)
             pieces.append(piece)
         groups.append(jnp.concatenate(pieces, axis=1))
-    state = jnp.concatenate(groups + [jnp.zeros((8, cells), F32)], axis=0)
+    state = jnp.concatenate(groups, axis=0)
     total = jnp.zeros((1, 1), F32)
     for s in range(2):
         high, low = halves(state)
@@ -263,7 +262,7 @@
         pairs += [(a.at[s], b.at[s]) for a, b in zip((w1h, w2h, b2h, w3h), (w1, w2, b2, w3))]
     copies = started(pairs, sems)
     refs = (w1m.at[2], w2m.at[2], b2m.at[2], w3m, b3m.at[2])
-    updated, logs = mid_update(u_in[...], refs, copies[:1], x_scr, p_scr)
+    updated, logs = mid_update(u_in[...], refs, copies[:1], x_scr, p_scr, 2048)
     awaited(copies[1:6])
     total = sum_in[0:1, 0:1] + const[0:1, 0:1] + logs
     high, low = halves(updated)
@@ -308,9 +307,10 @@
 def pack_kernel(images, packed):
     for i in range(8):
         rows = images[i]
-        wide = jnp.concatenate([rows[0:8], rows[8:16], rows[16:24], jnp.zeros((8, 32), F32)], axis=1)
+        wide = jnp.concatenate([rows[6 * j : 6 * j + 6] for j in range(4)], axis=1)
         for r in range(8):
-            packed[8 * r + i] = wide
+            for t in range(3):
+                packed[8 * r + i, t] = wide[2 * t : 2 * t + 2]
 
 
 def shapes(*items):
@@ -339,7 +339,7 @@
 
 def pack(images):
     return pl.pallas_call(
-        pack_kernel, in_specs=[VMEM], out_specs=VMEM, out_shape=jax.ShapeDtypeStruct((64, 8, 128), F32), name="pack"
+        pack_kernel, in_specs=[VMEM], out_specs=VMEM, out_shape=jax.ShapeDtypeStruct((64, 3, 2, 128), F32), name="pack"
     )(images.reshape(8, 24, 32))
 
 

time: 55.6 us -> 53.5 us (0.962)
  waiting for transfers between devices: 8.84 us -> 7.69 us
  Pallas kernels: 23.6 us -> 22.9 us
    all_to_all x1, waiting for transfers between devices: 8.83 us -> 7.68 us  [body(): slots = lax.all_to_all(pack(images), ('rows', 'chan'), 0, 0, tiled=True)]
    pallas_call x3, Pallas kernels: 21.9 us -> 21.2 us  [call(): pl.pallas_call(kernel, in_specs=specs, out_specs=out_specs or (VMEM,) * l...]
where the time goes in v3:
time: 53.5 us; the launch traced here: 53.2 us
  Pallas kernels  22.9 us (43%)
  starting transfers between devices  21.3 us (40%)
  waiting for transfers between devices  7.69 us (14%)
  local copies, waits for them, and re-layouts  0.68 us (1%)
  between operations  0.68 us (1%)
    pallas_call x3, Pallas kernels, call(): pl.pallas_call(kernel, in_specs=specs, out_specs=out_specs or (VMEM,) * l...  21.2 us
    all_to_all x1, starting transfers between devices, body(): slots = lax.all_to_all(pack(images), ('rows', 'chan'), 0, 0, tiled=True)  17.6 us
    all_to_all x1, waiting for transfers between devices, body(): slots = lax.all_to_all(pack(images), ('rows', 'chan'), 0, 0, tiled=True)  7.68 us
    all_to_all x1, starting transfers between devices, body(): latent_mid = lax.all_to_all(latent, 'chan', 0, 0, tiled=True)  3.68 us
    pallas_call x1, Pallas kernels, pack(): pl.pallas_call(pack_kernel, in_specs=[VMEM], out_specs=VMEM, out_shape=ja...  1.66 us
  transfers between devices with their start and end apart: 2, of which 1 were waited for; matrix products, arithmetic and copies ran while one was open for 0% of the time, Pallas kernels for 27%

profile of v3, /device:TPU:1, one launch (start us, length us, event | category | flops | bytes accessed | tf_op | source)
XLA Modules:
  0.0 53.2 jit_solution(11133186494936939034)
XLA Ops:
  0.6 1.7 %pack.1 = f32[64,3,2,128]{3,2,1,0:T(2,128)} custom-call(f32[8,24,32]{2,1,0:T(8,128)} %bitcast.16), custom_call_target="tpu_custom_call" | custom-call | tf_op jit(solution)/shard_map/pack/pallas_call | solution.py:341
  2.3 17.6 %all-to-all-start = ((f32[64,3,2,128]{3,2,1,0:T(2,128)}), f32[64,3,2,128]{3,2,1,0:T(2,128)S(1)}, u32[]{:S(2)}, u32[]{:S(2)}) async-start(f32[64,3,2,128]{3,2,1,0:T(2,128)} %pack.1), calls=%async_computation | async-start | bytes 393216 | tf_op jit(solution)/shard_map/all_to_all | solution.py:403
  19.9 6.5 %prep.1 = (bf16[3,32,96]{2,1,0:T(8,128)(2,1)S(1)}, f32[3,32,128]{2,1,0:T(8,128)S(1)}, bf16[3,512,144]{2,1,0:T(8,128)(2,1)S(1)}, bf16[3,512,512]{2,1,0:T(8,128)(2...) custom-call(f32[3,24]{1,0:T(4,128)} %shift_mid.1, ...), custom_call_target="tpu_custom_call" | custom-call | tf_op jit(solution)/shard_map/prep/pallas_call | solution.py:329
  26.4 7.7 %all-to-all-done.slots = f32[64,3,2,128]{3,2,1,0:T(2,128)S(1)} async-done(((f32[64,3,2,128]{3,2,1,0:T(2,128)}), f32[64,3,2,128]{3,2,1,0:T(2,128)S(1)}, u32[]{:S(2)}, u32[]{:S(2)}) %all-to-all-start) | async-done | bytes 196640 | tf_op jit(solution)/shard_map/all_to_all | solution.py:403
  34.1 7.0 %mid.1 = (f32[32,2048]{1,0:T(8,128)S(1)}, f32[8,128]{1,0:T(8,128)S(1)}, f32[8,16,128]{2,1,0:T(8,128)}) custom-call(s32[1]{0:T(128)} %bitcast.where, f32[64,3,2,128]{3,2,1,0:T(2,128)S(1)} %all-to-all-done.slots, bf16[3,32,96]{2,1,0:T(8,128)(2,1)S(1)} %get-tuple-element.22.a_mid, f32[3,32,128]{2,1,0:T(8,128)S(1)} %get-tuple-element.23.bu_mid, ...), custom_call_target="tpu_custom_call" | custom-call | tf_op jit(solution)/shard_map/mid/pallas_call | solution.py:329
  41.1 3.7 %all-to-all-start.1 = ((f32[8,16,128]{2,1,0:T(8,128)}), f32[8,16,128]{2,1,0:T(8,128)S(1)}, u32[]{:S(2)}, u32[]{:S(2)}) async-start(f32[8,16,128]{2,1,0:T(8,128)} %get-tuple-element.28), calls=%async_computation.1 | async-start | bytes 131072 | tf_op jit(solution)/shard_map/all_to_all | solution.py:409
  44.8 7.7 %top.1 = (f32[64,48]{1,0:T(8,128)}, f32[1]{0:T(128)}) custom-call(s32[1]{0:T(128)} %bitcast.where, f32[32,2048]{1,0:T(8,128)S(1)} %get-tuple-element.29.u_in, f32[8,128]{1,0:T(8,128)S(1)} %get-tuple-element.30.sum_in, f32[3,24,128]{2,1,0:T(8,128)S(1)} %get-tuple-element.24.b3.b3m, bf16[3,512,144]{2,1,0:T(8,128)(2,1)S(1)} %get-tuple-element.25.w1.w1m, ...), custom_call_target="tpu_custom_call" | custom-call | tf_op jit(solution)/shard_map/top/pallas_call | solution.py:329
  52.5 0.0 all-to-all-done.1
  52.5 0.7 %copy.26 = f32[8,12,1,32]{3,2,1,0:T(1,128)} copy(f32[8,12,1,32]{3,1,0,2:T(8,128)S(1)} %slice_bitcast_fusion) | data formatting | bytes 24576
  (1 shorter events, 0.0 us)
Async XLA Ops:
  2.3 31.8 %all-to-all-start = ((f32[64,3,2,128]{3,2,1,0:T(2,128)}), f32[64,3,2,128]{3,2,1,0:T(2,128)S(1)}, u32[]{:S(2)}, u32[]{:S(2)}) async-start(f32[64,3,2,128]{3,2,1,0:T(2,128)} %pack.1), calls=%async_computation | async-start | bytes 393216 | tf_op jit(solution)/shard_map/all_to_all | solution.py:403
  41.1 11.4 %all-to-all-start.1 = ((f32[8,16,128]{2,1,0:T(8,128)}), f32[8,16,128]{2,1,0:T(8,128)S(1)}, u32[]{:S(2)}, u32[]{:S(2)}) async-start(f32[8,16,128]{2,1,0:T(8,128)} %get-tuple-element.28), calls=%async_computation.1 | async-start | bytes 131072 | tf_op jit(solution)/shard_map/all_to_all | solution.py:409

commit v4 on v3

--- a/solution.py
+++ b/solution.py
@@ -10,6 +10,8 @@
 
 BF = jnp.bfloat16
 F32 = jnp.float32
+CHUNKS = 2
+SIZE = 2048 // CHUNKS
 log_two_pi = math.log(2.0 * math.pi)
 VMEM = pl.BlockSpec(memory_space=pltpu.VMEM)
 SMEM = pl.BlockSpec(memory_space=pltpu.SMEM)
@@ -151,31 +153,16 @@
     return jnp.where(inside, moved(x, dc), 0.0)
 
 
-def conditioner(q, extra, refs, copies, x_scr, p_scr, width, chunk):
+def conditioner(q, extra, refs, copies, width):
     cells = q.shape[1]
-    rows = q.shape[0]
     sides = [column_moved(q, dc, width) for dc in (-1, 0, 1)]
     blocks = [row_moved(side, dr, width) for dr in (-1, 0, 1) for side in sides]
-    if extra is not None:
-        blocks.append(extra)
-    x = jnp.concatenate(blocks, axis=0).astype(BF)
-    outs = []
-    if len(copies) > 1:
-        awaited(copies)
-    w1_ref, w2_ref, b2_ref, w3_ref, b3_ref = refs
-    w1, w2, b3 = w1_ref[...], w2_ref[...], b3_ref[...]
-    b2 = b2_ref[...]
-    if b2.shape[0] == 8:
-        b2 = jnp.concatenate([b2] * 16, axis=0).T
-    bias = tiled(b2, chunk)
-
-    n = cells // chunk
-    inner = [jnp.maximum(dot(w1, x[:, i * chunk : (i + 1) * chunk]), 0.0).astype(BF) for i in range(n)]
-    middle = [jnp.maximum(dot(w2, y) + bias, 0.0).astype(BF) for y in inner]
-    if len(copies) == 1:
-        awaited(copies)
-    outs = [dot(w3_ref[...], y) for y in middle]
-    p = outs[0] if len(outs) == 1 else jnp.concatenate(outs, axis=1)
+    x = jnp.concatenate(blocks + [extra], axis=0).astype(BF)
+    awaited(copies)
+    w1, w2, b2, w3, b3 = (ref[...] for ref in refs)
+    inner = jnp.maximum(dot(w1, x), 0.0).astype(BF)
+    middle = jnp.maximum(dot(w2, inner) + tiled(b2, cells), 0.0).astype(BF)
+    p = dot(w3, middle)
     n_out = p.shape[0] // 9
     out = tiled(b3, cells)
     for dc in (-1, 0, 1):
@@ -198,12 +185,85 @@
     return dot(a, jnp.concatenate(parts, axis=0)) + bias
 
 
-def mid_update(u, refs, copies, x_scr, p_scr, chunk=1024):
-    out = conditioner(u[:16], None, refs, copies, x_scr, p_scr, 32, chunk)
-    scale, logs = gate_of(out[:16])
-    logs = jnp.where(iota(logs.shape, 0) < 12, logs, 0.0)
-    updated = (u[16:] + out[8:]) * pltpu.roll(scale, 4, 0)
-    return updated, jnp.sum(logs, keepdims=True)
+def widened(chunks, c):
+    zeros = jnp.zeros((chunks[c].shape[0], 128), F32)
+    low = chunks[c - 1][:, -128:] if c else zeros
+    high = chunks[c + 1][:, :128] if c + 1 < CHUNKS else zeros
+    return jnp.concatenate([low, chunks[c], high], axis=1)
+
+
+def within(x):
+    return x[:, 128 : 128 + SIZE]
+
+
+def first_layer(u, c, w1):
+    wide = widened([x[:16] for x in u] + [None] * (CHUNKS - len(u)), c)
+    sides = [column_moved(wide, dc, 32) for dc in (-1, 0, 1)]
+    blocks = [within(moved(side, 32 * dr) if dr else side) for dr in (-1, 0, 1) for side in sides]
+    return jnp.maximum(dot(w1, jnp.concatenate(blocks, axis=0).astype(BF)), 0.0).astype(BF)
+
+
+def last_layer(p, c, b3):
+    wide = widened(p + [None] * (CHUNKS - len(p)), c)
+    out = tiled(b3, SIZE)
+    for dc in (-1, 0, 1):
+        part = None
+        for dr in (-1, 0, 1):
+            tap = 3 * (dr + 1) + dc + 1
+            term = wide[24 * tap : 24 * tap + 24]
+            term = moved(term, 32 * dr) if dr else term
+            part = term if part is None else part + term
+        out = out + within(column_moved(part, dc, 32))
+    return out
+
+
+def mid_layers(u, inner, refs, copies, after):
+    w2, bias, w3_ref, b3 = refs
+    p, made, total = [], [], None
+
+    def finish(c):
+        out = last_layer(p, c, b3)
+        scale, logs = gate_of(out[:16])
+        updated = (u[c][16:] + out[8:]) * pltpu.roll(scale, 4, 0)
+        made.append(after(jnp.concatenate([u[c][:16], updated], axis=0)))
+        return logs
+
+    middle = [jnp.maximum(dot(w2, x) + bias, 0.0).astype(BF) for x in inner]
+    awaited(copies)
+    for c in range(CHUNKS):
+        p.append(dot(w3_ref[...], middle[c]))
+        if c:
+            logs = finish(c - 1)
+            total = logs if total is None else total + logs
+    return made, total, finish
+
+
+def mid_steps(u, weights, copies, steps, mixes):
+    w1, w2, b2, w3, b3 = weights
+    inner = [first_layer(u, c, w1[steps[0]]) for c in range(CHUNKS)]
+    total = None
+    for n, s in enumerate(steps):
+        bias = tiled(jnp.concatenate([b2[s]] * 16, axis=0).T, SIZE)
+        made, logs, finish = mid_layers(u, inner, (w2[s], bias, w3.at[n], b3[s]), copies[n : n + 1], mixes[n])
+        inner = []
+        if n + 1 < len(steps):
+            for c in range(CHUNKS - 2):
+                inner.append(first_layer(made, c, w1[steps[n + 1]]))
+        logs = logs + finish(CHUNKS - 1)
+        total = logs if total is None else total + logs
+        if n + 1 < len(steps):
+            for c in range(CHUNKS - 2, CHUNKS):
+                inner.append(first_layer(made, c, w1[steps[n + 1]]))
+        u = made
+    return u, jnp.sum(jnp.where(iota(total.shape, 0) < 12, total, 0.0), keepdims=True)
+
+
+def next_mix(a, bu):
+    def mixed(state):
+        high, low = halves(state)
+        return mix(a, [high, low, high], tiled(bu, state.shape[1]))
+
+    return mixed
 
 
 def started(pairs, sems):
@@ -218,7 +278,7 @@
         copy.wait()
 
 
-def mid_kernel(where, slots, a_mid, bu_mid, b3, w1, w2, b2, w3h, u_out, sum_out, latent_out, x_scr, p_scr, w3, sems):
+def mid_kernel(where, slots, a_mid, bu_mid, b3, w1, w2, b2, w3h, u_out, sum_out, latent_out, w3, sems):
     copies = started([(w3h.at[s], w3.at[s]) for s in range(2)], sems)
     cells = 2048
     lane = iota((8, 128), 1) // 32
@@ -228,25 +288,20 @@
         for k in range(16):
             piece = None
             for j in range(4):
-                source = jnp.concatenate([slots[4 * k + j, t] for t in range(3)] + [jnp.zeros((2, 128), F32)], axis=0)
+                source = jnp.concatenate([slots[8 * ((4 * k + j) % 8) + (4 * k + j) // 8, t] for t in range(3)] + [jnp.zeros((2, 128), F32)], axis=0)
                 turn = (32 * (j - g)) % 128
                 source = pltpu.roll(source, turn, 1) if turn else source
                 piece = source if piece is None else jnp.where(lane == j, source, piece)
             pieces.append(piece)
         groups.append(jnp.concatenate(pieces, axis=1))
     state = jnp.concatenate(groups, axis=0)
-    total = jnp.zeros((1, 1), F32)
-    for s in range(2):
-        high, low = halves(state)
-        u = mix(a_mid[s], [high, low, high], tiled(bu_mid[s], cells))
-        updated, logs = mid_update(u, (w1.at[s], w2.at[s], b2.at[s], w3.at[s], b3.at[s]), copies[s : s + 1], x_scr, p_scr)
-        total = total + logs
-        state = jnp.concatenate([u[:16], updated], axis=0)
-    high, low = halves(state)
-    u = mix(a_mid[2], [high, low, high], tiled(bu_mid[2], cells))
-    u_out[...] = u
-    latent = jnp.where(iota((16, cells), 0) < 12, u[:16], 0.0)
-    total = total - 0.5 * jnp.sum(latent * latent, keepdims=True)
+    mixes = [next_mix(a_mid[s], bu_mid[s]) for s in range(3)]
+    u = [mixes[0](state[:, SIZE * c : SIZE * (c + 1)]) for c in range(CHUNKS)]
+    u, total = mid_steps(u, (w1, w2, b2, w3, b3), copies, (0, 1), mixes[1:])
+    for c in range(CHUNKS):
+        u_out[:, SIZE * c : SIZE * (c + 1)] = u[c]
+    squares = sum(x[:16] * x[:16] for x in u)
+    total = total - 0.5 * jnp.sum(jnp.where(iota(squares.shape, 0) < 12, squares, 0.0), keepdims=True)
     sum_out[...] = jnp.broadcast_to(total, (8, 128))
     own = u_out[0:16, pl.ds(pl.multiple_of(where[0] * 256, 256), 256)]
     for j in range(8):
@@ -255,14 +310,15 @@
 
 
 def top_kernel(where, u_in, sum_in, b3m, w1m, w2m, b2m, w3mh, w1h, w2h, b2h, w3h, *rest):
-    small_h, (latent_out, sum_out, x_scr, p_scr, xt_scr, pt_scr, w3m, w1, w2, b2, w3, *small, sems) = rest[:5], rest[5:]
+    small_h, (latent_out, sum_out, w3m, w1, w2, b2, w3, *small, sems) = rest[:5], rest[5:]
     a_top0, a_top1, bu_top, b3, const = small
-    pairs = [(w3mh.at[2], w3m)] + list(zip(small_h, small))
+    pairs = [(w3mh.at[2], w3m.at[0])] + list(zip(small_h, small))
     for s in range(2):
         pairs += [(a.at[s], b.at[s]) for a, b in zip((w1h, w2h, b2h, w3h), (w1, w2, b2, w3))]
     copies = started(pairs, sems)
-    refs = (w1m.at[2], w2m.at[2], b2m.at[2], w3m, b3m.at[2])
-    updated, logs = mid_update(u_in[...], refs, copies[:1], x_scr, p_scr, 2048)
+    u = [u_in[:, SIZE * c : SIZE * (c + 1)] for c in range(CHUNKS)]
+    updated, logs = mid_steps(u, (w1m, w2m, b2m, w3m, b3m), copies[:1], (2,), [lambda state: state[16:]])
+    updated = jnp.concatenate(updated, axis=1)
     awaited(copies[1:6])
     total = sum_in[0:1, 0:1] + const[0:1, 0:1] + logs
     high, low = halves(updated)
@@ -289,7 +345,7 @@
     u = mix(a_top0[...], parts + parts[:4], tiled(bu_top[0], 512))
     ones = (iota((8, 512), 0) == 0).astype(F32)
     for s in range(2):
-        out = conditioner(u[:24], ones, (w1.at[s], w2.at[s], b2.at[s], w3.at[s], b3.at[s]), copies[6 + 4 * s : 10 + 4 * s], xt_scr, pt_scr, 16, 512)
+        out = conditioner(u[:24], ones, (w1.at[s], w2.at[s], b2.at[s], w3.at[s], b3.at[s]), copies[6 + 4 * s : 10 + 4 * s], 16)
         scale, logs = gate_of(out[:24])
         total = total + jnp.sum(logs, keepdims=True)
         state = jnp.concatenate([u[:24], (u[24:] + out[24:]) * scale], axis=0)
@@ -310,7 +366,7 @@
         wide = jnp.concatenate([rows[6 * j : 6 * j + 6] for j in range(4)], axis=1)
         for r in range(8):
             for t in range(3):
-                packed[8 * r + i, t] = wide[2 * t : 2 * t + 2]
+                packed[8 * i + r, t] = wide[2 * t : 2 * t + 2]
 
 
 def shapes(*items):
@@ -361,9 +417,6 @@
     )
 
 
-MID_SCRATCH = (pltpu.VMEM((144, 2048), BF), pltpu.VMEM((216, 2048), F32))
-
-
 def mid(where, slots, prepared, third):
     a, bu, w1, w2, b2, b3 = (in_vmem(x) for x in prepared[:6])
     return call(
@@ -372,7 +425,7 @@
         [where, in_vmem(slots), a, bu, b3, w1, w2, b2, in_hbm(third)],
         [SMEM] + [VMEM] * 7 + [HBM],
         [pltpu.VMEM((32, 2048), F32), pltpu.VMEM((8, 128), F32), jax.ShapeDtypeStruct((8, 16, 128), F32)],
-        MID_SCRATCH + (pltpu.VMEM((2, 216, 512), BF), pltpu.SemaphoreType.DMA((2,))),
+        (pltpu.VMEM((2, 216, 512), BF), pltpu.SemaphoreType.DMA((2,))),
         limit=24 * 2**20,
     )
 
@@ -387,9 +440,8 @@
         + [in_hbm(x) for x in (third_m, w1, w2, b2, third, a0, a1, bu, b3, const)],
         [SMEM] + [VMEM] * 6 + [HBM] * 10,
         [jax.ShapeDtypeStruct((64, 48), F32), jax.ShapeDtypeStruct((1,), F32)],
-        MID_SCRATCH
-        + (
-            pltpu.VMEM((224, 512), BF), pltpu.VMEM((432, 512), F32), pltpu.VMEM((216, 512), BF),
+        (
+            pltpu.VMEM((1, 216, 512), BF),
             pltpu.VMEM((2, 512, 224), BF), pltpu.VMEM((2, 512, 512), BF), pltpu.VMEM((2, 512, 128), F32), pltpu.VMEM((2, 432, 512), BF),
             pltpu.VMEM((48, 192), BF), pltpu.VMEM((48, 144), BF), pltpu.VMEM((2, 48, 128), F32), pltpu.VMEM((2, 48, 128), F32), pltpu.VMEM((8, 128), F32),
             pltpu.SemaphoreType.DMA((14,)),
@@ -400,7 +452,7 @@
 
 
 def body(images, *params):
-    slots = lax.all_to_all(pack(images), ("rows", "chan"), 0, 0, tiled=True)
+    slots = lax.all_to_all(pack(images), ("chan", "rows"), 0, 0, tiled=True)
     third_mid = params[9].transpose(0, 1, 3, 2).reshape(3, 216, 512)
     third_top = params[20].transpose(0, 1, 3, 2).reshape(2, 432, 512)
     prepared = prep(params)

time: 53.5 us -> 53.3 us (level)
  starting transfers between devices: 21.3 us -> 22.8 us
  waiting for transfers between devices: 7.69 us -> 6.23 us
    all_to_all x1, starting transfers between devices: 3.68 us -> 5.14 us  [body(): latent_mid = lax.all_to_all(latent, 'chan', 0, 0, tiled=True)]
    all_to_all x1, waiting for transfers between devices: 7.68 us -> 6.22 us  [body(): slots = lax.all_to_all(pack(images), ('chan', 'rows'), 0, 0, tiled=True)]
where the time goes in v4:
time: 53.3 us; the launch traced here: 53 us
  starting transfers between devices  22.8 us (43%)
  Pallas kernels  22.7 us (43%)
  waiting for transfers between devices  6.23 us (12%)
  local copies, waits for them, and re-layouts  0.68 us (1%)
  between operations  0.68 us (1%)
    pallas_call x3, Pallas kernels, call(): pl.pallas_call(kernel, in_specs=specs, out_specs=out_specs or (VMEM,) * l...  21 us
    all_to_all x1, starting transfers between devices, body(): slots = lax.all_to_all(pack(images), ('chan', 'rows'), 0, 0, tiled=True)  17.6 us
    all_to_all x1, waiting for transfers between devices, body(): slots = lax.all_to_all(pack(images), ('chan', 'rows'), 0, 0, tiled=True)  6.22 us
    all_to_all x1, starting transfers between devices, body(): latent_mid = lax.all_to_all(latent, 'chan', 0, 0, tiled=True)  5.14 us
    pallas_call x1, Pallas kernels, pack(): pl.pallas_call(pack_kernel, in_specs=[VMEM], out_specs=VMEM, out_shape=ja...  1.66 us
  transfers between devices with their start and end apart: 2, of which 1 were waited for; matrix products, arithmetic and copies ran while one was open for 0% of the time, Pallas kernels for 27%

profile of v4, /device:TPU:1, one launch (start us, length us, event | category | flops | bytes accessed | tf_op | source)
XLA Modules:
  0.0 53.0 jit_solution(10251758841511743427)
XLA Ops:
  0.6 1.7 %pack.1 = f32[64,3,2,128]{3,2,1,0:T(2,128)} custom-call(f32[8,24,32]{2,1,0:T(8,128)} %bitcast.16), custom_call_target="tpu_custom_call" | custom-call | tf_op jit(solution)/shard_map/pack/pallas_call | solution.py:397
  2.3 17.6 %all-to-all-start = ((f32[64,3,2,128]{3,2,1,0:T(2,128)}), f32[64,3,2,128]{3,2,1,0:T(2,128)S(1)}, u32[]{:S(2)}, u32[]{:S(2)}) async-start(f32[64,3,2,128]{3,2,1,0:T(2,128)} %pack.1), calls=%async_computation | async-start | bytes 393216 | tf_op jit(solution)/shard_map/all_to_all | solution.py:455
  19.9 6.5 %prep.1 = (bf16[3,32,96]{2,1,0:T(8,128)(2,1)S(1)}, f32[3,32,128]{2,1,0:T(8,128)S(1)}, bf16[3,512,144]{2,1,0:T(8,128)(2,1)S(1)}, bf16[3,512,512]{2,1,0:T(8,128)(2...) custom-call(f32[3,24]{1,0:T(4,128)} %shift_mid.1, ...), custom_call_target="tpu_custom_call" | custom-call | tf_op jit(solution)/shard_map/prep/pallas_call | solution.py:385
  26.4 6.2 %all-to-all-done.slots = f32[64,3,2,128]{3,2,1,0:T(2,128)S(1)} async-done(((f32[64,3,2,128]{3,2,1,0:T(2,128)}), f32[64,3,2,128]{3,2,1,0:T(2,128)S(1)}, u32[]{:S(2)}, u32[]{:S(2)}) %all-to-all-start) | async-done | bytes 196640 | tf_op jit(solution)/shard_map/all_to_all | solution.py:455
  32.6 6.9 %mid.1 = (f32[32,2048]{1,0:T(8,128)S(1)}, f32[8,128]{1,0:T(8,128)S(1)}, f32[8,16,128]{2,1,0:T(8,128)}) custom-call(s32[1]{0:T(128)} %bitcast.where, f32[64,3,2,128]{3,2,1,0:T(2,128)S(1)} %all-to-all-done.slots, bf16[3,32,96]{2,1,0:T(8,128)(2,1)S(1)} %get-tuple-element.22.a_mid, f32[3,32,128]{2,1,0:T(8,128)S(1)} %get-tuple-element.23.bu_mid, ...), custom_call_target="tpu_custom_call" | custom-call | tf_op jit(solution)/shard_map/mid/pallas_call | solution.py:385
  39.5 5.1 %all-to-all-start.1 = ((f32[8,16,128]{2,1,0:T(8,128)}), f32[8,16,128]{2,1,0:T(8,128)S(1)}, u32[]{:S(2)}, u32[]{:S(2)}) async-start(f32[8,16,128]{2,1,0:T(8,128)} %get-tuple-element.28), calls=%async_computation.1 | async-start | bytes 131072 | tf_op jit(solution)/shard_map/all_to_all | solution.py:461
  44.7 7.6 %top.1 = (f32[64,48]{1,0:T(8,128)}, f32[1]{0:T(128)}) custom-call(s32[1]{0:T(128)} %bitcast.where, f32[32,2048]{1,0:T(8,128)S(1)} %get-tuple-element.29.u_in, f32[8,128]{1,0:T(8,128)S(1)} %get-tuple-element.30.sum_in, f32[3,24,128]{2,1,0:T(8,128)S(1)} %get-tuple-element.24.b3.b3m, bf16[3,512,144]{2,1,0:T(8,128)(2,1)S(1)} %get-tuple-element.25.w1.w1m, ...), custom_call_target="tpu_custom_call" | custom-call | tf_op jit(solution)/shard_map/top/pallas_call | solution.py:385
  52.3 0.0 all-to-all-done.1
  52.3 0.7 %copy.26 = f32[8,12,1,32]{3,2,1,0:T(1,128)} copy(f32[8,12,1,32]{3,1,0,2:T(8,128)S(1)} %slice_bitcast_fusion) | data formatting | bytes 24576
  (1 shorter events, 0.0 us)
Async XLA Ops:
  2.3 30.3 %all-to-all-start = ((f32[64,3,2,128]{3,2,1,0:T(2,128)}), f32[64,3,2,128]{3,2,1,0:T(2,128)S(1)}, u32[]{:S(2)}, u32[]{:S(2)}) async-start(f32[64,3,2,128]{3,2,1,0:T(2,128)} %pack.1), calls=%async_computation | async-start | bytes 393216 | tf_op jit(solution)/shard_map/all_to_all | solution.py:455
  39.5 12.8 %all-to-all-start.1 = ((f32[8,16,128]{2,1,0:T(8,128)}), f32[8,16,128]{2,1,0:T(8,128)S(1)}, u32[]{:S(2)}, u32[]{:S(2)}) async-start(f32[8,16,128]{2,1,0:T(8,128)} %get-tuple-element.28), calls=%async_computation.1 | async-start | bytes 131072 | tf_op jit(solution)/shard_map/all_to_all | solution.py:461

commit v5 on v4

--- a/solution.py
+++ b/solution.py
@@ -11,6 +11,10 @@
 BF = jnp.bfloat16
 F32 = jnp.float32
 CHUNKS = 2
+MID_ROWS = 512
+MID_OUT = 216
+TOP_ROWS = 256
+TOP_OUT = 216
 SIZE = 2048 // CHUNKS
 log_two_pi = math.log(2.0 * math.pi)
 VMEM = pl.BlockSpec(memory_space=pltpu.VMEM)
@@ -153,6 +157,10 @@
     return jnp.where(inside, moved(x, dc), 0.0)
 
 
+def in_rows(a, b, rows, finish):
+    return jnp.concatenate([finish(dot(a[k : k + rows], b), k) for k in range(0, a.shape[0], rows)], axis=0)
+
+
 def conditioner(q, extra, refs, copies, width):
     cells = q.shape[1]
     sides = [column_moved(q, dc, width) for dc in (-1, 0, 1)]
@@ -160,9 +168,9 @@
     x = jnp.concatenate(blocks + [extra], axis=0).astype(BF)
     awaited(copies)
     w1, w2, b2, w3, b3 = (ref[...] for ref in refs)
-    inner = jnp.maximum(dot(w1, x), 0.0).astype(BF)
-    middle = jnp.maximum(dot(w2, inner) + tiled(b2, cells), 0.0).astype(BF)
-    p = dot(w3, middle)
+    inner = in_rows(w1, x, TOP_ROWS, lambda y, k: jnp.maximum(y, 0.0).astype(BF))
+    middle = in_rows(w2, inner, TOP_ROWS, lambda y, k: jnp.maximum(y + tiled(b2[k : k + TOP_ROWS], cells), 0.0).astype(BF))
+    p = in_rows(w3, middle, TOP_OUT, lambda y, k: y)
     n_out = p.shape[0] // 9
     out = tiled(b3, cells)
     for dc in (-1, 0, 1):
@@ -200,7 +208,7 @@
     wide = widened([x[:16] for x in u] + [None] * (CHUNKS - len(u)), c)
     sides = [column_moved(wide, dc, 32) for dc in (-1, 0, 1)]
     blocks = [within(moved(side, 32 * dr) if dr else side) for dr in (-1, 0, 1) for side in sides]
-    return jnp.maximum(dot(w1, jnp.concatenate(blocks, axis=0).astype(BF)), 0.0).astype(BF)
+    return in_rows(w1, jnp.concatenate(blocks, axis=0).astype(BF), MID_ROWS, lambda y, k: jnp.maximum(y, 0.0).astype(BF))
 
 
 def last_layer(p, c, b3):
@@ -228,10 +236,12 @@
         made.append(after(jnp.concatenate([u[c][:16], updated], axis=0)))
         return logs
 
-    middle = [jnp.maximum(dot(w2, x) + bias, 0.0).astype(BF) for x in inner]
+    middle = [
+        in_rows(w2, x, MID_ROWS, lambda y, k: jnp.maximum(y + bias[k : k + MID_ROWS], 0.0).astype(BF)) for x in inner
+    ]
     awaited(copies)
     for c in range(CHUNKS):
-        p.append(dot(w3_ref[...], middle[c]))
+        p.append(in_rows(w3_ref[...], middle[c], MID_OUT, lambda y, k: y))
         if c:
             logs = finish(c - 1)
             total = logs if total is None else total + logs

time: 53.3 us -> 53 us (level)
  transfers between devices with their start and end apart: 2 -> 2, of which waited for: 1 -> 2; matrix products, arithmetic and copies ran while one was open for 0% -> 0% of each run, Pallas kernels for 27% -> 26%
where the time goes in v5:
time: 53 us; the launch traced here: 52.8 us
  starting transfers between devices  22.8 us (43%)
  Pallas kernels  22.2 us (42%)
  waiting for transfers between devices  6.48 us (12%)
  local copies, waits for them, and re-layouts  0.68 us (1%)
  between operations  0.66 us (1%)
    pallas_call x3, Pallas kernels, call(): pl.pallas_call(kernel, in_specs=specs, out_specs=out_specs or (VMEM,) * l...  20.5 us
    all_to_all x1, starting transfers between devices, body(): slots = lax.all_to_all(pack(images), ('chan', 'rows'), 0, 0, tiled=True)  17.6 us
    all_to_all x1, waiting for transfers between devices, body(): slots = lax.all_to_all(pack(images), ('chan', 'rows'), 0, 0, tiled=True)  6.22 us
    all_to_all x1, starting transfers between devices, body(): latent_mid = lax.all_to_all(latent, 'chan', 0, 0, tiled=True)  5.14 us
    pallas_call x1, Pallas kernels, pack(): pl.pallas_call(pack_kernel, in_specs=[VMEM], out_specs=VMEM, out_shape=ja...  1.66 us
  transfers between devices with their start and end apart: 2, of which 2 were waited for; matrix products, arithmetic and copies ran while one was open for 0% of the time, Pallas kernels for 26%

profile of v5, /device:TPU:1, one launch (start us, length us, event | category | flops | bytes accessed | tf_op | source)
XLA Modules:
  0.0 52.8 jit_solution(18343174025232153240)
XLA Ops:
  0.6 1.7 %pack.1 = f32[64,3,2,128]{3,2,1,0:T(2,128)} custom-call(f32[8,24,32]{2,1,0:T(8,128)} %bitcast.16), custom_call_target="tpu_custom_call" | custom-call | tf_op jit(solution)/shard_map/pack/pallas_call | solution.py:407
  2.3 17.6 %all-to-all-start = ((f32[64,3,2,128]{3,2,1,0:T(2,128)}), f32[64,3,2,128]{3,2,1,0:T(2,128)S(1)}, u32[]{:S(2)}, u32[]{:S(2)}) async-start(f32[64,3,2,128]{3,2,1,0:T(2,128)} %pack.1), calls=%async_computation | async-start | bytes 393216 | tf_op jit(solution)/shard_map/all_to_all | solution.py:465
  19.9 6.5 %prep.1 = (bf16[3,32,96]{2,1,0:T(8,128)(2,1)S(1)}, f32[3,32,128]{2,1,0:T(8,128)S(1)}, bf16[3,512,144]{2,1,0:T(8,128)(2,1)S(1)}, bf16[3,512,512]{2,1,0:T(8,128)(2...) custom-call(f32[3,24]{1,0:T(4,128)} %shift_mid.1, ...), custom_call_target="tpu_custom_call" | custom-call | tf_op jit(solution)/shard_map/prep/pallas_call | solution.py:395
  26.4 6.2 %all-to-all-done.slots = f32[64,3,2,128]{3,2,1,0:T(2,128)S(1)} async-done(((f32[64,3,2,128]{3,2,1,0:T(2,128)}), f32[64,3,2,128]{3,2,1,0:T(2,128)S(1)}, u32[]{:S(2)}, u32[]{:S(2)}) %all-to-all-start) | async-done | bytes 196640 | tf_op jit(solution)/shard_map/all_to_all | solution.py:465
  32.6 6.9 %mid.1 = (f32[32,2048]{1,0:T(8,128)S(1)}, f32[8,128]{1,0:T(8,128)S(1)}, f32[8,16,128]{2,1,0:T(8,128)}) custom-call(s32[1]{0:T(128)} %bitcast.where, f32[64,3,2,128]{3,2,1,0:T(2,128)S(1)} %all-to-all-done.slots, bf16[3,32,96]{2,1,0:T(8,128)(2,1)S(1)} %get-tuple-element.22.a_mid, f32[3,32,128]{2,1,0:T(8,128)S(1)} %get-tuple-element.23.bu_mid, ...), custom_call_target="tpu_custom_call" | custom-call | tf_op jit(solution)/shard_map/mid/pallas_call | solution.py:395
  39.5 5.1 %all-to-all-start.1 = ((f32[8,16,128]{2,1,0:T(8,128)}), f32[8,16,128]{2,1,0:T(8,128)S(1)}, u32[]{:S(2)}, u32[]{:S(2)}) async-start(f32[8,16,128]{2,1,0:T(8,128)} %get-tuple-element.28), calls=%async_computation.1 | async-start | bytes 131072 | tf_op jit(solution)/shard_map/all_to_all | solution.py:471
  44.7 7.2 %top.1 = (f32[64,48]{1,0:T(8,128)}, f32[1]{0:T(128)}) custom-call(s32[1]{0:T(128)} %bitcast.where, f32[32,2048]{1,0:T(8,128)S(1)} %get-tuple-element.29.u_in, f32[8,128]{1,0:T(8,128)S(1)} %get-tuple-element.30.sum_in, f32[3,24,128]{2,1,0:T(8,128)S(1)} %get-tuple-element.24.b3.b3m, bf16[3,512,144]{2,1,0:T(8,128)(2,1)S(1)} %get-tuple-element.25.w1.w1m, ...), custom_call_target="tpu_custom_call" | custom-call | tf_op jit(solution)/shard_map/top/pallas_call | solution.py:395
  51.8 0.3 all-to-all-done.1
  52.1 0.7 %copy.26 = f32[8,12,1,32]{3,2,1,0:T(1,128)} copy(f32[8,12,1,32]{3,1,0,2:T(8,128)S(1)} %slice_bitcast_fusion) | data formatting | bytes 24576
  (1 shorter events, 0.0 us)
Async XLA Ops:
  2.3 30.3 %all-to-all-start = ((f32[64,3,2,128]{3,2,1,0:T(2,128)}), f32[64,3,2,128]{3,2,1,0:T(2,128)S(1)}, u32[]{:S(2)}, u32[]{:S(2)}) async-start(f32[64,3,2,128]{3,2,1,0:T(2,128)} %pack.1), calls=%async_computation | async-start | bytes 393216 | tf_op jit(solution)/shard_map/all_to_all | solution.py:465
  39.5 12.6 %all-to-all-start.1 = ((f32[8,16,128]{2,1,0:T(8,128)}), f32[8,16,128]{2,1,0:T(8,128)S(1)}, u32[]{:S(2)}, u32[]{:S(2)}) async-start(f32[8,16,128]{2,1,0:T(8,128)} %get-tuple-element.28), calls=%async_computation.1 | async-start | bytes 131072 | tf_op jit(solution)/shard_map/all_to_all | solution.py:471
